TPU v7x, 8 devices: a whole 2x2x1 slice. The times are simulated.
8 devices in a mesh: part: 1 (over z), loc: 2 (over y), grp: 4 (over x, core).
Axes of the slice: x: 2, y: 2, z: 1, core: 2. Of those that a mesh axis runs over, the one named last changes fastest.
Arguments:
- x_tok: bfloat16 [2048, 2048], P(('part', 'grp', 'loc'))
- expert_ids: int32 [2048, 8], P(('part', 'grp', 'loc'))
- gate_val: float32 [2048, 8], P(('part', 'grp', 'loc'))
- w_gate: bfloat16 [64, 2048, 1024], P(('grp', 'loc'))
- w_up: bfloat16 [64, 2048, 1024], P(('grp', 'loc'))
- w_down: bfloat16 [64, 1024, 2048], P(('grp', 'loc'))
Outputs:
- output: bfloat16 [2048, 2048], P(('part', 'grp', 'loc'))
All inputs are finite; a program needn't handle non-finite values.
Results may differ from a plain program's by a relative error of at most 0.0123254.
Values are sent between devices in bfloat16 or wider.
A program may use at most 1 GiB of HBM per device.

v0:
```python
import jax
import jax.numpy as jnp
from jax import lax
from jax.sharding import PartitionSpec as P


def expert_rows(in_rows, row_ids, row_gate, w_gate, w_up, w_down, first_expert, capacity):
    n_rows, d_model = in_rows.shape
    top_k = row_ids.shape[1]
    n_local = w_gate.shape[0]
    local_ids = (row_ids - first_expert).reshape(-1)
    one_hot = (local_ids[:, None] == jnp.arange(n_local)[None, :]).astype(jnp.int32)
    position = jnp.sum(jnp.cumsum(one_hot, axis=0) * one_hot, axis=1) - 1
    is_valid = jnp.sum(one_hot, axis=1) > 0
    slot_ids = jnp.where(is_valid, local_ids * capacity + position, n_local * capacity)
    src_row = jnp.zeros(n_local * capacity, jnp.int32).at[slot_ids].set(jnp.arange(n_rows * top_k, dtype=jnp.int32) // top_k, mode="drop")
    src_gate = jnp.zeros(n_local * capacity, jnp.float32).at[slot_ids].set(row_gate.reshape(-1), mode="drop")
    packed = jnp.take(in_rows, src_row, axis=0).reshape(n_local, capacity, d_model)
    up_gate = jnp.einsum("ecd,edf->ecf", packed, w_gate, preferred_element_type=jnp.float32)
    up_lin = jnp.einsum("ecd,edf->ecf", packed, w_up, preferred_element_type=jnp.float32)
    hidden = (jax.nn.silu(up_gate) * up_lin).astype(jnp.bfloat16)
    out_rows = jnp.einsum("ecf,efd->ecd", hidden, w_down, preferred_element_type=jnp.float32)
    weighted = out_rows.reshape(n_local * capacity, d_model) * src_gate[:, None]
    return jax.ops.segment_sum(weighted, src_row, num_segments=n_rows)


def solution(mesh):
    n_grp = mesh.shape["grp"]
    n_loc = mesh.shape["loc"]
    tok_spec = P(("part", "grp", "loc"), None)
    w_spec = P(("grp", "loc"), None, None)

    def device_step(x_tok, expert_ids, gate_val, w_gate, w_up, w_down):
        tok_local, d_model = x_tok.shape
        top_k = expert_ids.shape[1]
        n_local = w_gate.shape[0]
        per_group = n_local * n_loc
        tokens_part = tok_local * n_grp * n_loc
        capacity = 8 * (tokens_part * top_k // (4 * per_group * n_grp) + 1)
        first_expert = (lax.axis_index("grp") * n_loc + lax.axis_index("loc")) * n_local
        owner_grp = expert_ids // per_group
        grp_mask = owner_grp[None, :, :] == jnp.arange(n_grp)[:, None, None]
        grp_hit = jnp.any(grp_mask, axis=2)
        send_rows = jnp.where(grp_hit[:, :, None], x_tok[None], jnp.zeros((), x_tok.dtype))
        send_ids = jnp.where(grp_mask, expert_ids[None], -1)
        send_gate = jnp.where(grp_mask, gate_val[None], 0.0)
        n_relay = n_grp * tok_local
        relay_rows = lax.all_to_all(send_rows, "grp", 0, 0, tiled=True).reshape(n_relay, d_model)
        relay_ids = lax.all_to_all(send_ids, "grp", 0, 0, tiled=True).reshape(n_relay, top_k)
        relay_gate = lax.all_to_all(send_gate, "grp", 0, 0, tiled=True).reshape(n_relay, top_k)
        owner_loc = (relay_ids % per_group) // n_local
        loc_mask = (owner_loc[None] == jnp.arange(n_loc)[:, None, None]) & (relay_ids >= 0)[None]
        loc_hit = jnp.any(loc_mask, axis=2)
        fan_rows = jnp.where(loc_hit[:, :, None], relay_rows[None], jnp.zeros((), relay_rows.dtype))
        fan_ids = jnp.where(loc_mask, relay_ids[None], -1)
        fan_gate = jnp.where(loc_mask, relay_gate[None], 0.0)
        got_rows = lax.all_to_all(fan_rows, "loc", 0, 0, tiled=True).reshape(n_loc * n_relay, d_model)
        got_ids = lax.all_to_all(fan_ids, "loc", 0, 0, tiled=True).reshape(n_loc * n_relay, top_k)
        got_gate = lax.all_to_all(fan_gate, "loc", 0, 0, tiled=True).reshape(n_loc * n_relay, top_k)
        row_sums = expert_rows(got_rows, got_ids, got_gate, w_gate, w_up, w_down, first_expert, capacity)
        back_sums = lax.all_to_all(row_sums.reshape(n_loc, n_relay, d_model), "loc", 0, 0, tiled=True)
        group_part = jnp.sum(back_sums, axis=0).astype(jnp.bfloat16).reshape(n_grp, tok_local, d_model)
        home_parts = lax.all_to_all(group_part, "grp", 0, 0, tiled=True)
        return jnp.sum(home_parts, axis=0, dtype=jnp.float32).astype(jnp.bfloat16)

    return jax.shard_map(device_step, mesh=mesh, in_specs=(tok_spec, tok_spec, tok_spec, w_spec, w_spec, w_spec), out_specs=tok_spec, check_vma=False)
```

profile of v0, /device:TPU:0, one launch (start us, length us, event | category | flops | bytes accessed | tf_op | source)
XLA Modules:
  0.0 695.1 jit_solution(5287877454070272791)
XLA Ops:
  0.0 0.7 add_select_fusion.3
  0.7 1.3 fusion.23
  2.0 4.6 all-to-all-start
  6.6 1.3 fusion.21
  8.0 2.4 all-to-all-done
  10.4 3.3 all-to-all-start.4
  13.7 0.6 fusion.17
  14.3 3.0 all-to-all-done.4
  17.3 3.3 all-to-all-start.1
  20.6 3.6 broadcast_select_fusion.6
  24.2 0.3 all-to-all-done.1
  24.5 4.9 all-to-all-start.2
  29.5 0.6 fusion.15
  30.1 0.3 copy.21
  30.5 0.5 sub.54
  31.0 0.5 sub.53
  31.5 0.1 copy.24
  31.6 0.1 fusion.9
  31.7 0.3 reduce-window.9
  32.1 0.2 copy.25
  32.3 0.6 fusion.8
  32.9 44.3 %all-to-all-done.2 = bf16[4,256,2048]{2,1,0:T(8,128)(2,1)} async-done(((bf16[4,256,2048]{2,1,0:T(8,128)(2,1)}), bf16[4,256,2048]{2,1,0:T(8,128)(2,1)}, u32[]{:S(2)}, u32[]{:S(2)}) %all-to-all-start.2) | async-done | bytes 4194336 | tf_op jit(solution)/shard_map/all_to_all | solution.py:48
  77.3 3.3 all-to-all-start.5
  80.6 6.1 broadcast_select_fusion.5
  86.7 0.0 all-to-all-done.5
  86.7 6.9 all-to-all-start.3
  93.6 0.3 copy.22
  94.0 0.5 mul.44
  94.5 0.3 copy.26
  94.9 0.5 reshape.180
  95.4 0.1 compare_select_fusion
  95.5 60.4 %scatter_custom_fusion = s32[4160]{0:T(1024)S(1)} fusion(s32[16384]{0:T(1024)S(1)} %bitcast.44, s32[16384]{0:T(1024)S(1)} %add_select_fusion, s32[]{:T(128)} %constant.86.clone.1), kind=kCustom, calls=%fused_computation.69 | custom fusion | bytes 16644 | tf_op jit(solution)/shard_map/scatter | solution.py:16
  155.9 0.0 copy-start
  155.9 0.1 broadcast_in_dim.144
  156.0 60.9 %scatter_custom_fusion.1 = f32[4160]{0:T(1024)} fusion(s32[16384]{0:T(1024)S(1)} %bitcast.45, f32[16384]{0:T(1024)S(1)} %reshape.180, f32[]{:T(128)} %constant.85.clone.1), kind=kCustom, calls=%fused_computation.67 | custom fusion | bytes 16644 | tf_op jit(solution)/shard_map/scatter | solution.py:17
  216.9 0.0 all-to-all-done.3
  216.9 37.4 %gather_fusion = bf16[4160,2048]{1,0:T(8,128)(2,1)} fusion(bf16[2048,2048]{1,0:T(8,128)(2,1)} %bitcast.6, s32[5120]{0:T(1024)S(1)} %pad_clamp_fusion), kind=kCustom, calls=%fused_computation | custom fusion | bytes 34095360 | tf_op jit(solution)/shard_map/jit(_take)/gather | solution.py:18
  254.4 0.0 copy-done
  254.4 31.5 %fusion = f32[8,520,1024]{2,1,0:T(8,128)} fusion(bf16[8,2048,1024]{2,1,0:T(8,128)(2,1)} %param.10, bf16[8,520,2048]{2,1,0:T(8,128)(2,1)} %bitcast.35, pred[8,520]{1,0:T(8,128)(4,1)S(1)} %broadcast_in_dim.144), kind=kOutput, calls=%fused_computation.7 | convolution fusion | flops 17456824320 | bytes 67637312 | tf_op jit(solution)/shard_map/ecd,edf->ecf/dot_general | solution.py:20
  285.8 0.0 copy-start.1
  285.8 52.0 %fusion.6 = f32[8,520,2048]{2,1,0:T(8,128)} fusion(bf16[8,1024,2048]{2,1,0:T(8,128)(2,1)} %param.11, f32[8,520,1024]{2,1,0:T(8,128)} %fusion, bf16[8,2048,1024]{2,1,0:T(8,128)(2,1)} %param.9, bf16[8,520,2048]{2,1,0:T(8,128)(2,1)} %bitcast.36, pred[8,520]{1,0:T(8,128)(4,1)S(1)} %broadcast_in_dim.144), kind=kOutput, calls=%fused_computation.15 | convolution fusion | flops 34930688000 | bytes 135270464 | tf_op jit(solution)/shard_map/ecf,efd->ecd/dot_general | solution.py:22
  337.8 0.0 copy-done.1
  337.8 23.3 %bitcast_multiply_fusion = f32[4160,2048]{1,0:T(8,128)} fusion(f32[8,520,2048]{2,1,0:T(8,128)} %fusion.6, f32[4160]{0:T(1024)S(1)} %copy-done.1), kind=kLoop, calls=%fused_computation.4 | loop fusion | flops 8519680 | bytes 68174080 | tf_op jit(solution)/shard_map/mul | solution.py:23
  361.1 65.3 %scatter_custom_fusion.2 = f32[2048,2048]{1,0:T(8,128)} fusion(s32[4160]{0:T(1024)} %copy-done, f32[4160,2048]{1,0:T(8,128)} %bitcast_multiply_fusion, f32[]{:T(128)} %constant.85.clone.1), kind=kCustom, calls=%fused_computation.11 | custom fusion | flops 8519680 | bytes 16777728 | tf_op jit(solution)/shard_map/scatter-add | solution.py:24
  426.4 200.1 %all_to_all.40 = f32[2,1024,2048]{2,1,0:T(8,128)} all-to-all(f32[2,1024,2048]{2,1,0:T(8,128)} %bitcast.34), channel_id=1, replica_groups=mesh['part'=1,'loc'=2,'grp'=4] {'loc'}, dimensions={0} | all-to-all | bytes 33554432 | tf_op jit(solution)/shard_map/all_to_all | solution.py:61
  626.5 10.8 %reduce_sum.41 = bf16[1024,2048]{1,0:T(8,128)(2,1)} reduce(f32[2,1024,2048]{2,1,0:T(8,128)} %all_to_all.40, f32[]{:T(128)} %constant.85.clone.1), dimensions={0}, to_apply=%region_9.10 | reduce | flops 2097152 | bytes 20971524 | tf_op jit(solution)/shard_map/reduce_sum | solution.py:62
  637.3 53.5 %all_to_all.41 = bf16[4,256,2048]{2,1,0:T(8,128)(2,1)} all-to-all(bf16[4,256,2048]{2,1,0:T(8,128)(2,1)} %bitcast.37), channel_id=1, replica_groups=mesh['part'=1,'loc'=2,'grp'=4] {'grp'}, dimensions={0} | all-to-all | bytes 8388608 | tf_op jit(solution)/shard_map/all_to_all | solution.py:63
  690.9 4.2 reduce_sum.42
  (14 shorter events, 0.2 us)
Async XLA Ops:
  2.0 8.3 %all-to-all-start = ((s32[4,256,8]{1,2,0:T(8,128)}), s32[4,256,8]{1,2,0:T(8,128)S(1)}, u32[]{:S(2)}, u32[]{:S(2)}) async-start(s32[4,256,8]{1,2,0:T(8,128)} %fusion.23), calls=%async_computation | async-start | bytes 65536 | tf_op jit(solution)/shard_map/all_to_all | solution.py:49
  10.4 7.0 %all-to-all-start.4 = ((f32[4,256,8]{1,2,0:T(8,128)}), f32[4,256,8]{1,2,0:T(8,128)S(1)}, u32[]{:S(2)}, u32[]{:S(2)}) async-start(f32[4,256,8]{1,2,0:T(8,128)} %fusion.21), calls=%async_computation.4 | async-start | bytes 65536 | tf_op jit(solution)/shard_map/all_to_all | solution.py:50
  17.3 7.2 %all-to-all-start.1 = ((s32[2,1024,8]{1,2,0:T(8,128)}), s32[2,1024,8]{1,2,0:T(8,128)S(1)}, u32[]{:S(2)}, u32[]{:S(2)}) async-start(s32[2,1024,8]{1,2,0:T(8,128)} %fusion.17), calls=%async_computation.1 | async-start | bytes 131072 | tf_op jit(solution)/shard_map/all_to_all | solution.py:58
  24.5 52.7 %all-to-all-start.2 = ((bf16[4,256,2048]{2,1,0:T(8,128)(2,1)}), bf16[4,256,2048]{2,1,0:T(8,128)(2,1)}, u32[]{:S(2)}, u32[]{:S(2)}) async-start(bf16[4,256,2048]{2,1,0:T(8,128)(2,1)} %broadcast_select_fusion.6), calls=%async_computation.2 | async-start | bytes 8388608 | tf_op jit(solution)/shard_map/all_to_all | solution.py:48
  77.3 9.4 %all-to-all-start.5 = ((f32[2,1024,8]{1,2,0:T(8,128)}), f32[2,1024,8]{1,2,0:T(8,128)S(1)}, u32[]{:S(2)}, u32[]{:S(2)}) async-start(f32[2,1024,8]{1,2,0:T(8,128)} %fusion.15), calls=%async_computation.5 | async-start | bytes 131072 | tf_op jit(solution)/shard_map/all_to_all | solution.py:59
  86.7 130.2 %all-to-all-start.3 = ((bf16[2,1024,2048]{2,1,0:T(8,128)(2,1)}), bf16[2,1024,2048]{2,1,0:T(8,128)(2,1)}, u32[]{:S(2)}, u32[]{:S(2)}) async-start(bf16[2,1024,2048]{2,1,0:T(8,128)(2,1)} %broadcast_select_fusion.5), calls=%async_computation.3 | async-start | bytes 16777216 | tf_op jit(solution)/shard_map/all_to_all | solution.py:57
  155.9 98.5 %copy-start = (s32[4160]{0:T(1024)}, s32[4160]{0:T(1024)S(1)}, u32[]{:S(2)}) copy-start(s32[4160]{0:T(1024)S(1)} %scatter_custom_fusion) | copy-start | bytes 49924
  285.8 52.0 %copy-start.1 = (f32[4160]{0:T(1024)S(1)}, f32[4160]{0:T(1024)}, u32[]{:S(2)}) copy-start(f32[4160]{0:T(1024)} %scatter_custom_fusion.1) | copy-start | bytes 49924
where the time goes:
time: 697 us; the launch traced here: 695 us
  blocking collectives  254 us (36%)
  local copies, waits for them, and re-layouts  162 us (23%)
  other arithmetic  119 us (17%)
  matrix products  83.5 us (12%)
  waiting for transfers between devices  50.1 us (7%)
  starting transfers between devices  26.2 us (4%)
    all_to_all x1, blocking collectives, device_step(): lax.all_to_all(row_sums.reshape(n_loc, n_relay, d_model), 'loc', 0, 0, ti...  200 us
    scatter-add x1, other arithmetic, expert_rows(): return jax.ops.segment_sum(weighted, src_row, num_segments=n_rows)  65.3 us
    scatter x1, local copies, waits for them, and re-layouts, expert_rows(): jnp.zeros(n_local * capacity, jnp.float32).at[slot_ids]  60.9 us
    scatter x1, local copies, waits for them, and re-layouts, expert_rows(): jnp.zeros(n_local * capacity, jnp.int32).at[slot_ids]  60.4 us
    all_to_all x1, blocking collectives, device_step(): home_parts = lax.all_to_all(group_part, 'grp', 0, 0, tiled=True)  53.5 us
    dot_general x1, matrix products, expert_rows(): jnp.einsum('ecf,efd->ecd', hidden, w_down, preferred_element_type=jnp.flo...  52 us
    all_to_all x1, waiting for transfers between devices, device_step(): lax.all_to_all(send_rows, 'grp', 0, 0, tiled=True).reshape(n_relay, d_model)  44.3 us
    gather x1, local copies, waits for them, and re-layouts, expert_rows(): jnp.take(in_rows, src_row, axis=0).reshape(n_local, capacity, d_model)  37.4 us
  transfers between devices with their start and end apart: 6, of which 4 were waited for; matrix products, arithmetic and copies ran while one was open for 20% of the time, Pallas kernels for 0%

commit v1 on v0

v1 whole, which is shorter than its diff:
```python
import functools

import jax
import jax.numpy as jnp
from jax import lax
from jax.experimental import pallas as pl
from jax.experimental.pallas import tpu as pltpu
from jax.sharding import PartitionSpec as P


MESH = pl.DeviceIdType.MESH
LANES = 128
TILE = 256
PAD = 16
STEP = 16
SLOTS = 2


def share_kernel(n_grp, n_loc, mine_ref, all_ref, send_sem, recv_sem):
    grp, loc = lax.axis_index("grp"), lax.axis_index("loc")
    n_dev = n_grp * n_loc

    def peer(r):
        return {"grp": grp ^ (r % n_grp), "loc": loc ^ (r // n_grp)}

    barrier = pltpu.get_barrier_semaphore()
    for r in range(1, n_dev):
        pl.semaphore_signal(barrier, inc=1, device_id=peer(r), device_id_type=MESH)
    pl.semaphore_wait(barrier, n_dev - 1)
    copies = []
    for r in range(1, n_dev):
        copy = pltpu.make_async_remote_copy(
            src_ref=mine_ref, dst_ref=all_ref.at[r], send_sem=send_sem.at[r], recv_sem=recv_sem.at[r], device_id=peer(r), device_id_type=MESH
        )
        copy.start()
        copies.append(copy)
    all_ref[0] = mine_ref[...]
    for copy in copies:
        copy.wait()


def zero_acc(acc):
    def zero(i, c):
        acc[pl.ds(i * 16, 16)] = jnp.zeros((16,) + acc.shape[1:], jnp.float32)
        return c

    lax.fori_loop(0, acc.shape[0] // 16, zero, 0)


def gather_rows(list_ref, at, first, x_ref, xs, stride):
    chunks = x_ref.shape[1]
    for k in range(STEP):
        row = x_ref[list_ref[at + (first + k)]]
        xs[pl.ds(first + k, chunks, stride=stride), :] = row.astype(jnp.float32)


def scatter_rows(list_ref, at, gate_ref, gate_at, first, ot, acc, stride):
    chunks = acc.shape[1]
    for k0 in range(0, STEP, 4):
        slots, sums = [], []
        for k in range(k0, k0 + 4):
            s = list_ref[at + (first + k)]
            slots.append(s)
            sums.append(acc[s] + gate_ref[gate_at + s] * ot[pl.ds(first + k, chunks, stride=stride), :])
        for s, v in zip(slots, sums):
            acc[s] = v


def pass_kernel(n_local, list_len, n_pad, row_block, x_places, out_places, cnt_ref, list_ref, gate_ref, *refs):
    n_x, n_out = len(x_places), len(out_places)
    stride = row_block + 4
    x_hbm, (wg_hbm, wu_hbm, wd_hbm), refs = refs[:n_x], refs[n_x:n_x + 3], refs[n_x + 3:]
    outs, (x_ref, acc, xs, xg, hid, wg_ref, wu_ref, wd_ref, x_sem, w_sem, out_sem) = refs[:n_out], refs[n_out:]
    d_ff, d_model = wd_ref.shape[1:]

    def weights(e, slot):
        return [
            pltpu.make_async_copy(wg_hbm.at[e], wg_ref.at[slot], w_sem.at[slot, 0]),
            pltpu.make_async_copy(wu_hbm.at[e], wu_ref.at[slot], w_sem.at[slot, 1]),
            pltpu.make_async_copy(wd_hbm.at[e], wd_ref.at[slot], w_sem.at[slot, 2]),
        ]

    x_copies = [pltpu.make_async_copy(src, x_ref.at[pl.ds(at, src.shape[0])], x_sem.at[k]) for k, (src, at) in enumerate(zip(x_hbm, x_places))]
    for copy in x_copies:
        copy.start()
    for e in range(SLOTS):
        for copy in weights(e, e):
            copy.start()
    zero_acc(acc)
    for copy in x_copies:
        copy.wait()

    def expert(e, carry):
        slot = lax.rem(e, SLOTS)
        n = cnt_ref[e]
        now = weights(e, slot)
        now[0].wait()
        now[1].wait()
        now[2].wait()

        def block(b, c):
            base = b * row_block
            at = e * list_len + base
            steps = (jnp.minimum(row_block, n - base) + STEP - 1) // STEP

            def gather(q, c):
                gather_rows(list_ref, at, q * STEP, x_ref, xs, stride)
                return c

            lax.fori_loop(0, steps, gather, 0)
            for j in range(d_model // LANES):
                xg[:, j * LANES:(j + 1) * LANES] = xs[pl.ds(j * stride, row_block), :].astype(jnp.bfloat16)
            for q in range(d_ff // TILE):
                cols = slice(q * TILE, (q + 1) * TILE)
                u = jnp.dot(xg[...], wg_ref[slot, :, cols], preferred_element_type=jnp.float32)
                v = jnp.dot(xg[...], wu_ref[slot, :, cols], preferred_element_type=jnp.float32)
                hid[:, cols] = (jax.nn.silu(u) * v).astype(jnp.bfloat16)
            for q in range(d_model // TILE):
                o = jnp.dot(hid[...], wd_ref[slot, :, q * TILE:(q + 1) * TILE], preferred_element_type=jnp.float32)
                for k in range(TILE // LANES):
                    xs[pl.ds((q * (TILE // LANES) + k) * stride, row_block), :] = o[:, k * LANES:(k + 1) * LANES]

            def scatter(q, c):
                scatter_rows(list_ref, at, gate_ref, e * n_pad, q * STEP, xs, acc, stride)
                return c

            lax.fori_loop(0, steps, scatter, 0)
            return c

        lax.fori_loop(0, (n + row_block - 1) // row_block, block, 0)

        @pl.when(e + SLOTS < n_local)
        def _():
            for copy in weights(e + SLOTS, slot):
                copy.start()

        return carry

    lax.fori_loop(0, n_local, expert, 0)
    out_copies = [pltpu.make_async_copy(acc.at[pl.ds(at, ref.shape[0])], ref, out_sem.at[k]) for k, (ref, at) in enumerate(zip(outs, out_places))]
    for copy in out_copies:
        copy.start()
    for copy in out_copies:
        copy.wait()


def solution(mesh):
    n_grp = mesh.shape["grp"]
    n_loc = mesh.shape["loc"]
    n_dev = n_grp * n_loc
    tok_spec = P(("part", "grp", "loc"), None)
    w_spec = P(("grp", "loc"), None, None)

    def swap_grp(a, bits):
        return lax.ppermute(a, "grp", [(i, i ^ bits) for i in range(n_grp)])

    def swap_loc(a):
        return lax.ppermute(a, "loc", [(i, i ^ 1) for i in range(n_loc)])

    def swap_diag(a):
        pairs = [(l * n_grp + g, (l ^ 1) * n_grp + (g ^ 2)) for l in range(n_loc) for g in range(n_grp)]
        return lax.ppermute(a, ("loc", "grp"), pairs)

    def device_step(x_tok, expert_ids, gate_val, w_gate, w_up, w_down):
        tok_local, d_model = x_tok.shape
        d_ff = w_gate.shape[2]
        chunks = d_model // LANES
        n_local = w_gate.shape[0]
        per_group = n_local * n_loc
        n_tok = tok_local * n_dev
        top_k = expert_ids.shape[1]
        capacity = 8 * (n_tok * top_k // (4 * per_group * n_grp) + 1)
        me = lax.axis_index("grp") * n_loc + lax.axis_index("loc")

        meta = jnp.concatenate([expert_ids.astype(jnp.float32).T, gate_val.T], axis=0)
        meta_all = pl.pallas_call(
            functools.partial(share_kernel, n_grp, n_loc),
            out_shape=jax.ShapeDtypeStruct((n_dev,) + meta.shape, jnp.float32),
            in_specs=[pl.BlockSpec(memory_space=pltpu.VMEM)],
            out_specs=pl.BlockSpec(memory_space=pltpu.VMEM),
            scratch_shapes=[pltpu.SemaphoreType.DMA((n_dev,)), pltpu.SemaphoreType.DMA((n_dev,))],
            compiler_params=pltpu.CompilerParams(collective_id=0, has_side_effects=True),
            name="share",
        )(meta)
        mid = tok_local // 2
        low, high = (x_tok[h * mid:(h + 1) * mid].reshape(mid, chunks, LANES) for h in range(2))
        low, high, meta_all = lax.optimization_barrier((low, high, meta_all))

        y_low = swap_loc(low)
        c_low = swap_grp(low, 1)
        yc_low = swap_grp(y_low, 1)
        y_high = swap_loc(high)
        x_low = swap_grp(low, 2)
        x_high = swap_grp(high, 2)
        d_low = swap_loc(x_low)
        late, y_low = lax.optimization_barrier((high, y_low))
        d_high = swap_diag(late)
        parts = {
            0: [low, high],
            1: [c_low, swap_grp(high, 1)],
            2: [x_low, x_high],
            3: [swap_grp(x_low, 1), swap_grp(x_high, 1)],
            4: [y_low, y_high],
            5: [yc_low, swap_grp(y_high, 1)],
            6: [d_low, d_high],
            7: [swap_grp(d_low, 1), swap_grp(d_high, 1)],
        }

        cube = meta_all.transpose(1, 0, 2).reshape(2 * top_k, 2, 2, 2, 2, mid)
        near_meta = cube[:, :, 0, :, 0].reshape(2 * top_k, -1)
        far_meta = jnp.concatenate([cube[:, :, 1].reshape(2 * top_k, 2, 4, mid), cube[:, :, 0, :, 1]], axis=2).reshape(2 * top_k, -1)
        any_spec = pl.BlockSpec(memory_space=pl.ANY)
        piece = jax.ShapeDtypeStruct((mid, chunks, LANES), jnp.float32)

        def run_pass(homes, meta, row_block, before=None):
            blocks = [(k + dy * n_grp, h) for dy in range(n_loc) for k, h in homes]
            n_rows = len(blocks) * mid
            n_pad = n_rows + PAD
            list_len = -(-min(capacity, n_rows) // row_block) * row_block
            ids = meta[:top_k].astype(jnp.int32)
            gates = meta[top_k:]
            match = ids[None] == jnp.arange(n_local)[:, None, None] + me * n_local
            hit = jnp.any(match, axis=1)
            gate_of = jnp.sum(jnp.where(match, gates[None], 0.0), axis=1)
            gate_of = jnp.pad(gate_of, ((0, 0), (0, PAD))).reshape(-1)
            rank = jnp.cumsum(hit.astype(jnp.int32), axis=1)
            count = rank[:, -1]
            place = jnp.arange(list_len)[None, :]
            rows = jnp.sum((rank[:, None, :] <= place[:, :, None]).astype(jnp.int32), axis=2)
            rows = jnp.where(place < count[:, None], rows, n_rows + place % PAD).reshape(-1)

            x_parts = [parts[r][h] for r, h in blocks]
            x_places = [p * mid for p in range(len(blocks))]
            out_places = x_places[len(homes):] + x_places[:len(homes)]
            stride = row_block + 4
            if before is not None:
                count, before = lax.optimization_barrier((count, before))
            run = pl.pallas_call(
                functools.partial(pass_kernel, n_local, list_len, n_pad, row_block, x_places, out_places),
                grid_spec=pltpu.PrefetchScalarGridSpec(
                    num_scalar_prefetch=3,
                    grid=(),
                    in_specs=[any_spec] * (len(x_parts) + 3),
                    out_specs=[any_spec] * len(out_places),
                    scratch_shapes=[
                        pltpu.VMEM((n_pad, chunks, LANES), jnp.bfloat16),
                        pltpu.VMEM((n_pad, chunks, LANES), jnp.float32),
                        pltpu.VMEM((chunks * stride, LANES), jnp.float32),
                        pltpu.VMEM((row_block, d_model), jnp.bfloat16),
                        pltpu.VMEM((row_block, d_ff), jnp.bfloat16),
                        pltpu.VMEM((SLOTS, d_model, d_ff), jnp.bfloat16),
                        pltpu.VMEM((SLOTS, d_model, d_ff), jnp.bfloat16),
                        pltpu.VMEM((SLOTS, d_ff, d_model), jnp.bfloat16),
                        pltpu.SemaphoreType.DMA((len(x_parts),)),
                        pltpu.SemaphoreType.DMA((SLOTS, 3)),
                        pltpu.SemaphoreType.DMA((len(out_places),)),
                    ],
                ),
                out_shape=[piece] * len(out_places),
                compiler_params=pltpu.CompilerParams(vmem_limit_bytes=62_000_000),
                cost_estimate=pl.CostEstimate(flops=25 * 10**9, bytes_accessed=110 * 10**6, transcendentals=0),
            )
            outs = run(count, rows, gate_of, *x_parts, w_gate, w_up, w_down)
            pieces = {home: (outs[i], outs[len(homes) + i]) for i, home in enumerate(homes)}
            return {**(before or {}), **pieces}

        near, far = [(0, 0), (1, 0)], [(2, 0), (2, 1), (3, 0), (3, 1), (0, 1), (1, 1)]
        pieces = run_pass(near, near_meta, 96)
        pieces = run_pass(far, far_meta, 208, pieces)

        totals = [None, None]
        for k, h in near + [(2, 0), (2, 1), (3, 0), (3, 1), (1, 1), (0, 1)]:
            send, keep = pieces[k, h]
            mixed = (keep + swap_loc(send)).astype(jnp.bfloat16)
            back = (swap_grp(mixed, k) if k else mixed).astype(jnp.float32)
            totals[h] = back if totals[h] is None else totals[h] + back
        y = jnp.concatenate(totals, axis=0).astype(jnp.bfloat16)
        return y.reshape(tok_local, d_model)

    return jax.shard_map(device_step, mesh=mesh, in_specs=(tok_spec, tok_spec, tok_spec, w_spec, w_spec, w_spec), out_specs=tok_spec, check_vma=False)
```

time: 697 us -> 316 us (0.45)
  blocking collectives: 254 us -> 0 us
  local copies, waits for them, and re-layouts: 162 us -> 6.56 us
  waiting for transfers between devices: 50.1 us -> 157 us
  other arithmetic: 119 us -> 17.8 us
  Pallas kernels: 0 us -> 95.4 us
  matrix products: 83.5 us -> 0 us
  starting transfers between devices: 26.2 us -> 38.2 us
    all_to_all x2 -> x0, blocking collectives: 254 us -> none  [the longest x1 200 us: device_step(): lax.all_to_all(row_sums.reshape(n_loc, n_relay, d_model), 'loc', 0, 0, ti...]
    ppermute x0 -> x28, waiting for transfers between devices: none -> 157 us  [the longest x11 151 us: swap_loc(): return lax.ppermute(a, 'loc', [(i, i ^ 1) for i in range(n_loc)])]
    scatter x2 -> x0, local copies, waits for them, and re-layouts: 121 us -> none  [the longest x1 60.9 us: expert_rows(): jnp.zeros(n_local * capacity, jnp.float32).at[slot_ids]]
    pallas_call x0 -> x3, Pallas kernels: none -> 95.4 us  [the longest x2 86.9 us: run_pass(): outs = run(count, rows, gate_of, *x_parts, w_gate, w_up, w_down)]
    dot_general x2 -> x0, matrix products: 83.5 us -> none  [the longest x1 52 us: expert_rows(): jnp.einsum('ecf,efd->ecd', hidden, w_down, preferred_element_type=jnp.flo...]
    scatter-add x1 -> x0, other arithmetic: 65.3 us -> none  [expert_rows(): return jax.ops.segment_sum(weighted, src_row, num_segments=n_rows)]
    all_to_all x6 -> x0, waiting for transfers between devices: 50.1 us -> none  [the longest x1 44.3 us: device_step(): lax.all_to_all(send_rows, 'grp', 0, 0, tiled=True).reshape(n_relay, d_model)]
    ppermute x0 -> x28, starting transfers between devices: none -> 38.2 us  [the longest x16 25.4 us: swap_grp(): return lax.ppermute(a, 'grp', [(i, i ^ bits) for i in range(n_grp)])]
  transfers between devices with their start and end apart: 6 -> 28, of which waited for: 4 -> 11; matrix products, arithmetic and copies ran while one was open for 20% -> 6% of each run, Pallas kernels for 0% -> 28%
where the time goes in v1:
time: 316 us; the launch traced here: 315 us
  waiting for transfers between devices  157 us (50%)
  Pallas kernels  95.4 us (30%)
  starting transfers between devices  38.2 us (12%)
  other arithmetic  17.8 us (6%)
  local copies, waits for them, and re-layouts  6.56 us (2%)
    ppermute x11, waiting for transfers between devices, swap_loc(): return lax.ppermute(a, 'loc', [(i, i ^ 1) for i in range(n_loc)])  151 us
    pallas_call x2, Pallas kernels, run_pass(): outs = run(count, rows, gate_of, *x_parts, w_gate, w_up, w_down)  86.9 us
    ppermute x16, starting transfers between devices, swap_grp(): return lax.ppermute(a, 'grp', [(i, i ^ bits) for i in range(n_grp)])  25.4 us
    ppermute x11, starting transfers between devices, swap_loc(): return lax.ppermute(a, 'loc', [(i, i ^ 1) for i in range(n_loc)])  10.4 us
    pallas_call x1, Pallas kernels, device_step(): pl.pallas_call(functools.partial(share_kernel, n_grp, n_loc), out_shape=j...  8.5 us
  transfers between devices with their start and end apart: 28, of which 11 were waited for; matrix products, arithmetic and copies ran while one was open for 6% of the time, Pallas kernels for 28%

profile of v1, /device:TPU:0, one launch (start us, length us, event | category | flops | bytes accessed | tf_op | source)
XLA Modules:
  0.0 315.0 jit_solution(14669019438633867907)
XLA Ops:
  0.0 0.7 convert_bitcast_fusion.2
  0.7 1.3 pad_maximum_fusion.2.mine_ref
  2.0 8.5 %share.1 = f32[8,16,256]{2,1,0:T(8,128)} custom-call(f32[16,256]{1,0:T(8,128)} %pad_maximum_fusion.2.mine_ref), custom_call_target="tpu_custom_call" | custom-call | tf_op jit(solution)/shard_map/share/pallas_call | solution.py:176
  10.5 1.3 slice_bitcast_fusion
  12.1 1.5 collective-permute-start.6
  13.6 1.5 collective-permute-start.1
  15.1 0.6 collective-permute-start.15
  15.6 0.2 collective-permute-start.10
  15.9 1.0 reshape.142
  17.1 1.1 reduce-window.16
  18.2 0.2 slice_reduce_fusion.1
  18.6 0.2 slice_reduce_fusion.2.cnt_ref
  18.7 1.2 convert_reduce_fusion.1
  20.1 0.2 compare_reduce_fusion
  20.3 0.2 fusion
  20.5 0.7 reshape.146.gate_ref
  21.2 0.7 reshape.145.gate_ref
  22.0 0.7 select_n.49.list_ref
  22.7 2.3 reduce-window.14
  24.9 0.3 slice_reduce_fusion
  25.2 0.2 reduce-window.15
  25.5 0.2 slice_reduce_fusion.3.cnt_ref
  25.7 2.7 collective-permute-done.1.refs_2_
  28.4 0.5 collective-permute-start.7
  28.9 2.4 collective-permute-start.12
  31.3 7.8 %collective-permute-done.15.refs_10_ = bf16[128,16,128]{2,1,0:T(8,128)(2,1)S(1)} collective-permute-done((bf16[128,16,128]{2,1,0:T(8,128)(2,1)S(1)}, bf16[128,16,128]{2,1,0:T(8,128)(2,1)S(1)}, u32[]{:S(2)}, u32[]{:S(2)}) %collective-permute-start.15) | collective-permute-done | bytes 524320 | tf_op jit(solution)/shard_map/ppermute | solution.py:158
  39.1 2.4 collective-permute-start.11
  41.5 3.8 %convert_reduce_fusion = s32[8,624]{1,0:T(8,128)S(1)} fusion(s32[8,1536]{1,0:T(8,128)S(1)} %bitcast.63), kind=kLoop, calls=%fused_computation | loop fusion | flops 22998144 | bytes 69120 | tf_op jit(solution)/shard_map/reduce_sum | solution.py:229
  45.4 0.7 select_n.53.list_ref
  46.1 0.5 collective-permute-start.16
  46.6 15.1 %collective-permute-done.11.refs_6_ = bf16[128,16,128]{2,1,0:T(8,128)(2,1)} collective-permute-done((bf16[128,16,128]{2,1,0:T(8,128)(2,1)S(1)}, bf16[128,16,128]{2,1,0:T(8,128)(2,1)}, u32[]{:S(2)}, u32[]{:S(2)}) %collective-permute-start.11) | collective-permute-done | bytes 524320 | tf_op jit(solution)/shard_map/ppermute | solution.py:158
  61.7 0.5 collective-permute-start.13
  62.2 38.9 %shard_map.64 = (f32[128,16,128]{2,1,0:T(8,128)}, f32[128,16,128]{2,1,0:T(8,128)}, f32[128,16,128]{2,1,0:T(8,128)}, f32[128,16,128]{2,1,0:T(8,128)}) custom-call(s32[8]{0:T(128)} %copy-done.11, s32[4608]{0:T(1024)} %select_n.49.list_ref, f32[4224]{0:T(1024)} %reshape.145.gate_ref, bf16[128,16,128]{2,1,0:T(8,128)(2,1)} %bitcast.48, ...), custom_call_target="tpu_custom_call" | custom-call | flops 24999999488 | bytes 110000000 | tf_op jit(solution)/shard_map/pallas_call | solution.py:263
  101.2 1.2 collective-permute-start.4
  102.5 48.0 %shard_map.65 = (f32[128,16,128]{2,1,0:T(8,128)}, f32[128,16,128]{2,1,0:T(8,128)}, f32[128,16,128]{2,1,0:T(8,128)}, f32[128,16,128]{2,1,0:T(8,128)}, f32[128,16,...) custom-call(s32[8]{0:T(128)} %copy-done.12, ...), custom_call_target="tpu_custom_call" | custom-call | flops 24999999488 | bytes 110000000 | tf_op jit(solution)/shard_map/pallas_call | solution.py:263
  150.5 0.8 collective-permute-start.17
  151.2 1.3 collective-permute-start.19
  152.5 0.7 collective-permute-start.21
  153.3 1.3 collective-permute-start.23
  154.6 0.7 collective-permute-start.25
  155.3 0.1 add_convert_fusion.8
  155.4 17.8 %collective-permute-done.17 = f32[128,16,128]{2,1,0:T(8,128)S(1)} collective-permute-done((f32[128,16,128]{2,1,0:T(8,128)}, f32[128,16,128]{2,1,0:T(8,128)S(1)}, u32[]{:S(2)}, u32[]{:S(2)}) %collective-permute-start.17) | collective-permute-done | bytes 1048608 | tf_op jit(solution)/shard_map/ppermute | solution.py:158
  173.2 1.4 add_convert_fusion.7
  174.6 21.1 %collective-permute-done.19 = f32[128,16,128]{2,1,0:T(8,128)S(1)} collective-permute-done((f32[128,16,128]{2,1,0:T(8,128)}, f32[128,16,128]{2,1,0:T(8,128)S(1)}, u32[]{:S(2)}, u32[]{:S(2)}) %collective-permute-start.19) | collective-permute-done | bytes 1048608 | tf_op jit(solution)/shard_map/ppermute | solution.py:158
  195.7 1.4 add_convert_fusion.6
  197.0 21.1 %collective-permute-done.21 = f32[128,16,128]{2,1,0:T(8,128)S(1)} collective-permute-done((f32[128,16,128]{2,1,0:T(8,128)}, f32[128,16,128]{2,1,0:T(8,128)S(1)}, u32[]{:S(2)}, u32[]{:S(2)}) %collective-permute-start.21) | collective-permute-done | bytes 1048608 | tf_op jit(solution)/shard_map/ppermute | solution.py:158
  218.1 7.2 %collective-permute-start.5 = (bf16[128,16,128]{2,1,0:T(8,128)(2,1)S(1)}, bf16[128,16,128]{2,1,0:T(8,128)(2,1)S(1)}, u32[]{:S(2)}, u32[]{:S(2)}) collective-permute-start(bf16[128,16,128]{2,1,0:T(8,128)(2,1)S(1)} %add_convert_fusion.8), channel_id=1, source_target_pairs={{0,1},{1,0},{2,3},{3,2},{4,5},{5,4},{6,7},{7,6}} | collective-permute-start | bytes 1572872 | tf_op jit(solution)/shard_map/ppermute | solution.py:155
  225.3 1.4 add_convert_fusion.4
  226.7 13.9 %collective-permute-done.23 = f32[128,16,128]{2,1,0:T(8,128)S(1)} collective-permute-done((f32[128,16,128]{2,1,0:T(8,128)}, f32[128,16,128]{2,1,0:T(8,128)S(1)}, u32[]{:S(2)}, u32[]{:S(2)}) %collective-permute-start.23) | collective-permute-done | bytes 1048608 | tf_op jit(solution)/shard_map/ppermute | solution.py:158
  240.6 3.9 %collective-permute-start.18 = (bf16[128,16,128]{2,1,0:T(8,128)(2,1)S(1)}, bf16[128,16,128]{2,1,0:T(8,128)(2,1)S(1)}, u32[]{:S(2)}, u32[]{:S(2)}) collective-permute-start(bf16[128,16,128]{2,1,0:T(8,128)(2,1)S(1)} %add_convert_fusion.7), channel_id=1, source_target_pairs={{0,2},{1,3},{2,0},{3,1},{4,6},{5,7},{6,4},{7,5}} | collective-permute-start | bytes 1572872 | tf_op jit(solution)/shard_map/ppermute | solution.py:155
  244.5 18.6 %collective-permute-done.25 = f32[128,16,128]{2,1,0:T(8,128)S(1)} collective-permute-done((f32[128,16,128]{2,1,0:T(8,128)}, f32[128,16,128]{2,1,0:T(8,128)S(1)}, u32[]{:S(2)}, u32[]{:S(2)}) %collective-permute-start.25) | collective-permute-done | bytes 1048608 | tf_op jit(solution)/shard_map/ppermute | solution.py:158
  263.1 2.5 collective-permute-start.20
  265.6 0.1 add_convert_fusion.3
  265.7 0.1 add_convert_fusion.2
  265.9 19.7 %collective-permute-done.3 = f32[128,16,128]{2,1,0:T(8,128)S(1)} collective-permute-done((f32[128,16,128]{2,1,0:T(8,128)S(1)}, f32[128,16,128]{2,1,0:T(8,128)S(1)}, u32[]{:S(2)}, u32[]{:S(2)}) %collective-permute-start.3) | collective-permute-done | bytes 1048608 | tf_op jit(solution)/shard_map/ppermute | solution.py:158
  285.6 3.9 %collective-permute-start.22 = (bf16[128,16,128]{2,1,0:T(8,128)(2,1)S(1)}, bf16[128,16,128]{2,1,0:T(8,128)(2,1)S(1)}, u32[]{:S(2)}, u32[]{:S(2)}) collective-permute-start(bf16[128,16,128]{2,1,0:T(8,128)(2,1)S(1)} %add_convert_fusion.4), channel_id=1, source_target_pairs={{0,2},{1,3},{2,0},{3,1},{4,6},{5,7},{6,4},{7,5}} | collective-permute-start | bytes 1572872 | tf_op jit(solution)/shard_map/ppermute | solution.py:155
  289.4 4.7 %collective-permute-start.24 = (bf16[128,16,128]{2,1,0:T(8,128)(2,1)S(1)}, bf16[128,16,128]{2,1,0:T(8,128)(2,1)S(1)}, u32[]{:S(2)}, u32[]{:S(2)}) collective-permute-start(bf16[128,16,128]{2,1,0:T(8,128)(2,1)S(1)} %add_convert_fusion.3), channel_id=1, source_target_pairs={{0,3},{1,2},{2,1},{3,0},{4,7},{5,6},{6,5},{7,4}} | collective-permute-start | bytes 1572872 | tf_op jit(solution)/shard_map/ppermute | solution.py:155
  294.1 0.3 add_convert_fusion.5
  294.4 0.1 copy.30
  294.6 13.4 %collective-permute-done.27 = f32[128,16,128]{2,1,0:T(8,128)S(1)} collective-permute-done((f32[128,16,128]{2,1,0:T(8,128)}, f32[128,16,128]{2,1,0:T(8,128)S(1)}, u32[]{:S(2)}, u32[]{:S(2)}) %collective-permute-start.27) | collective-permute-done | bytes 1048608 | tf_op jit(solution)/shard_map/ppermute | solution.py:158
  308.0 5.4 %collective-permute-done.24 = bf16[128,16,128]{2,1,0:T(8,128)(2,1)S(1)} collective-permute-done((bf16[128,16,128]{2,1,0:T(8,128)(2,1)S(1)}, bf16[128,16,128]{2,1,0:T(8,128)(2,1)S(1)}, u32[]{:S(2)}, u32[]{:S(2)}) %collective-permute-start.24) | collective-permute-done | bytes 524320 | tf_op jit(solution)/shard_map/ppermute | solution.py:155
  313.5 0.3 add_convert_fusion
  313.8 0.1 copy.29
  313.9 1.1 pad_maximum_fusion
  (77 shorter events, 1.1 us)
Async XLA Ops:
  11.9 89.2 %copy-start = (bf16[16,8,16,128]{3,2,1,0:T(8,128)(2,1)}, bf16[16,8,16,128]{3,2,1,0:T(8,128)(2,1)S(1)}, u32[]{:S(2)}) copy-start(bf16[16,8,16,128]{3,2,1,0:T(8,128)(2,1)S(1)} %copy.22) | copy-start | bytes 1572868
  12.1 50.1 %copy-start.1 = (bf16[16,8,16,128]{3,2,1,0:T(8,128)(2,1)}, bf16[16,8,16,128]{3,2,1,0:T(8,128)(2,1)S(1)}, u32[]{:S(2)}) copy-start(bf16[16,8,16,128]{3,2,1,0:T(8,128)(2,1)S(1)} %copy.21) | copy-start | bytes 1572868
  12.1 16.8 %collective-permute-start.6 = (bf16[128,16,128]{2,1,0:T(8,128)(2,1)S(1)}, bf16[128,16,128]{2,1,0:T(8,128)(2,1)S(1)}, u32[]{:S(2)}, u32[]{:S(2)}) collective-permute-start(bf16[128,16,128]{2,1,0:T(8,128)(2,1)S(1)} %bitcast.45), channel_id=1, source_target_pairs={{0,2},{1,3},{2,0},{3,1},{4,6},{5,7},{6,4},{7,5}} | collective-permute-start | bytes 1572872 | tf_op jit(solution)/shard_map/ppermute | solution.py:155
  13.6 14.8 %collective-permute-start.1 = (bf16[128,16,128]{2,1,0:T(8,128)(2,1)S(1)}, bf16[128,16,128]{2,1,0:T(8,128)(2,1)S(1)}, u32[]{:S(2)}, u32[]{:S(2)}) collective-permute-start(bf16[128,16,128]{2,1,0:T(8,128)(2,1)S(1)} %bitcast.46), channel_id=1, source_target_pairs={{0,4},{4,0},{1,5},{5,1},{2,6},{6,2},{3,7},{7,3}} | collective-permute-start | bytes 1572872 | tf_op jit(solution)/shard_map/ppermute | solution.py:158
  15.1 16.3 %collective-permute-start = (bf16[128,16,128]{2,1,0:T(8,128)(2,1)S(1)}, bf16[128,16,128]{2,1,0:T(8,128)(2,1)}, u32[]{:S(2)}, u32[]{:S(2)}) collective-permute-start(bf16[128,16,128]{2,1,0:T(8,128)(2,1)S(1)} %bitcast.47), channel_id=1, source_target_pairs={{0,1},{1,0},{2,3},{3,2},{4,5},{5,4},{6,7},{7,6}} | collective-permute-start | bytes 1572872 | tf_op jit(solution)/shard_map/ppermute | solution.py:155
  15.1 24.1 %collective-permute-start.15 = (bf16[128,16,128]{2,1,0:T(8,128)(2,1)S(1)}, bf16[128,16,128]{2,1,0:T(8,128)(2,1)S(1)}, u32[]{:S(2)}, u32[]{:S(2)}) collective-permute-start(bf16[128,16,128]{2,1,0:T(8,128)(2,1)S(1)} %bitcast.40), channel_id=1, source_target_pairs={{0,4},{4,0},{1,5},{5,1},{2,6},{6,2},{3,7},{7,3}} | collective-permute-start | bytes 1572872 | tf_op jit(solution)/shard_map/ppermute | solution.py:158
  15.6 30.4 %collective-permute-start.10 = (bf16[128,16,128]{2,1,0:T(8,128)(2,1)S(1)}, bf16[128,16,128]{2,1,0:T(8,128)(2,1)S(1)}, u32[]{:S(2)}, u32[]{:S(2)}) collective-permute-start(bf16[128,16,128]{2,1,0:T(8,128)(2,1)S(1)} %bitcast.41), channel_id=1, source_target_pairs={{0,1},{1,0},{2,3},{3,2},{4,5},{5,4},{6,7},{7,6}} | collective-permute-start | bytes 1572872 | tf_op jit(solution)/shard_map/ppermute | solution.py:155
  18.7 43.5 %copy-start.11 = (s32[8]{0:T(128)}, s32[8]{0:T(128)S(1)}, u32[]{:S(2)}) copy-start(s32[8]{0:T(128)S(1)} %slice_reduce_fusion.2.cnt_ref) | copy-start | bytes 100
  25.7 75.4 %copy-start.12 = (s32[8]{0:T(128)}, s32[8]{0:T(128)S(1)}, u32[]{:S(2)}) copy-start(s32[8]{0:T(128)S(1)} %slice_reduce_fusion.3.cnt_ref) | copy-start | bytes 100
  28.4 33.8 %copy-start.10 = (bf16[128,16,128]{2,1,0:T(8,128)(2,1)}, bf16[128,16,128]{2,1,0:T(8,128)(2,1)S(1)}, u32[]{:S(2)}) copy-start(bf16[128,16,128]{2,1,0:T(8,128)(2,1)S(1)} %collective-permute-done.1.refs_2_) | copy-start | bytes 1572868
  28.4 17.7 %collective-permute-start.7 = (bf16[128,16,128]{2,1,0:T(8,128)(2,1)S(1)}, bf16[128,16,128]{2,1,0:T(8,128)(2,1)}, u32[]{:S(2)}, u32[]{:S(2)}) collective-permute-start(bf16[128,16,128]{2,1,0:T(8,128)(2,1)S(1)} %bitcast.42), channel_id=1, source_target_pairs={{0,2},{1,3},{2,0},{3,1},{4,6},{5,7},{6,4},{7,5}} | collective-permute-start | bytes 1572872 | tf_op jit(solution)/shard_map/ppermute | solution.py:155
  28.9 72.2 %copy-start.7 = (bf16[128,16,128]{2,1,0:T(8,128)(2,1)}, bf16[128,16,128]{2,1,0:T(8,128)(2,1)S(1)}, u32[]{:S(2)}) copy-start(bf16[128,16,128]{2,1,0:T(8,128)(2,1)S(1)} %collective-permute-done.6.refs_0_) | copy-start | bytes 1572868
  28.9 32.7 %collective-permute-start.12 = (bf16[128,16,128]{2,1,0:T(8,128)(2,1)S(1)}, bf16[128,16,128]{2,1,0:T(8,128)(2,1)}, u32[]{:S(2)}, u32[]{:S(2)}) collective-permute-start(bf16[128,16,128]{2,1,0:T(8,128)(2,1)S(1)} %bitcast.43), channel_id=1, source_target_pairs={{0,6},{1,7},{2,4},{3,5},{4,2},{5,3},{6,0},{7,1}} | collective-permute-start | bytes 1572872 | tf_op jit(solution)/shard_map/ppermute | solution.py:162
  31.3 30.8 %collective-permute-start.2 = (bf16[128,16,128]{2,1,0:T(8,128)(2,1)S(1)}, bf16[128,16,128]{2,1,0:T(8,128)(2,1)}, u32[]{:S(2)}, u32[]{:S(2)}) collective-permute-start(bf16[128,16,128]{2,1,0:T(8,128)(2,1)S(1)} %collective-permute-done.1.refs_2_), channel_id=1, source_target_pairs={{0,1},{1,0},{2,3},{3,2},{4,5},{5,4},{6,7},{7,6}} | collective-permute-start | bytes 1572872 | tf_op jit(solution)/shard_map/ppermute | solution.py:155
  39.1 62.0 %copy-start.8 = (bf16[128,16,128]{2,1,0:T(8,128)(2,1)}, bf16[128,16,128]{2,1,0:T(8,128)(2,1)S(1)}, u32[]{:S(2)}) copy-start(bf16[128,16,128]{2,1,0:T(8,128)(2,1)S(1)} %collective-permute-done.15.refs_10_) | copy-start | bytes 1572868
  39.1 22.5 %collective-permute-start.11 = (bf16[128,16,128]{2,1,0:T(8,128)(2,1)S(1)}, bf16[128,16,128]{2,1,0:T(8,128)(2,1)}, u32[]{:S(2)}, u32[]{:S(2)}) collective-permute-start(bf16[128,16,128]{2,1,0:T(8,128)(2,1)S(1)} %collective-permute-done.6.refs_0_), channel_id=1, source_target_pairs={{0,4},{4,0},{1,5},{5,1},{2,6},{6,2},{3,7},{7,3}} | collective-permute-start | bytes 1572872 | tf_op jit(solution)/shard_map/ppermute | solution.py:158
  46.1 55.1 %copy-start.9 = (bf16[128,16,128]{2,1,0:T(8,128)(2,1)}, bf16[128,16,128]{2,1,0:T(8,128)(2,1)S(1)}, u32[]{:S(2)}) copy-start(bf16[128,16,128]{2,1,0:T(8,128)(2,1)S(1)} %collective-permute-done.10.refs_5_) | copy-start | bytes 1572868
  46.1 55.1 %collective-permute-start.8 = (bf16[128,16,128]{2,1,0:T(8,128)(2,1)S(1)}, bf16[128,16,128]{2,1,0:T(8,128)(2,1)}, u32[]{:S(2)}, u32[]{:S(2)}) collective-permute-start(bf16[128,16,128]{2,1,0:T(8,128)(2,1)S(1)} %collective-permute-done.6.refs_0_), channel_id=1, source_target_pairs={{0,1},{1,0},{2,3},{3,2},{4,5},{5,4},{6,7},{7,6}} | collective-permute-start | bytes 1572872 | tf_op jit(solution)/shard_map/ppermute | solution.py:155
  46.1 56.4 %collective-permute-start.16 = (bf16[128,16,128]{2,1,0:T(8,128)(2,1)S(1)}, bf16[128,16,128]{2,1,0:T(8,128)(2,1)}, u32[]{:S(2)}, u32[]{:S(2)}) collective-permute-start(bf16[128,16,128]{2,1,0:T(8,128)(2,1)S(1)} %collective-permute-done.15.refs_10_), channel_id=1, source_target_pairs={{0,1},{1,0},{2,3},{3,2},{4,5},{5,4},{6,7},{7,6}} | collective-permute-start | bytes 1572872 | tf_op jit(solution)/shard_map/ppermute | solution.py:155
  61.6 40.8 %collective-permute-start.9 = (bf16[128,16,128]{2,1,0:T(8,128)(2,1)}, bf16[128,16,128]{2,1,0:T(8,128)(2,1)}, u32[]{:S(2)}, u32[]{:S(2)}) collective-permute-start(bf16[128,16,128]{2,1,0:T(8,128)(2,1)} %collective-permute-done.7.refs_1_), channel_id=1, source_target_pairs={{0,1},{1,0},{2,3},{3,2},{4,5},{5,4},{6,7},{7,6}} | collective-permute-start | bytes 1572872 | tf_op jit(solution)/shard_map/ppermute | solution.py:155
  61.7 40.8 %collective-permute-start.13 = (bf16[128,16,128]{2,1,0:T(8,128)(2,1)}, bf16[128,16,128]{2,1,0:T(8,128)(2,1)}, u32[]{:S(2)}, u32[]{:S(2)}) collective-permute-start(bf16[128,16,128]{2,1,0:T(8,128)(2,1)} %collective-permute-done.11.refs_6_), channel_id=1, source_target_pairs={{0,1},{1,0},{2,3},{3,2},{4,5},{5,4},{6,7},{7,6}} | collective-permute-start | bytes 1572872 | tf_op jit(solution)/shard_map/ppermute | solution.py:155
  62.2 40.3 %collective-permute-start.14 = (bf16[128,16,128]{2,1,0:T(8,128)(2,1)}, bf16[128,16,128]{2,1,0:T(8,128)(2,1)}, u32[]{:S(2)}, u32[]{:S(2)}) collective-permute-start(bf16[128,16,128]{2,1,0:T(8,128)(2,1)} %collective-permute-done.12.refs_7_), channel_id=1, source_target_pairs={{0,1},{1,0},{2,3},{3,2},{4,5},{5,4},{6,7},{7,6}} | collective-permute-start | bytes 1572872 | tf_op jit(solution)/shard_map/ppermute | solution.py:155
  101.2 54.1 %copy-start.4 = (f32[128,16,128]{2,1,0:T(8,128)S(1)}, f32[128,16,128]{2,1,0:T(8,128)}, u32[]{:S(2)}) copy-start(f32[128,16,128]{2,1,0:T(8,128)} %get-tuple-element.41) | copy-start | bytes 3145732
  101.2 72.0 %copy-start.13 = (f32[128,16,128]{2,1,0:T(8,128)S(1)}, f32[128,16,128]{2,1,0:T(8,128)}, u32[]{:S(2)}) copy-start(f32[128,16,128]{2,1,0:T(8,128)} %get-tuple-element.40) | copy-start | bytes 3145732
  101.2 53.3 %collective-permute-start.4 = (f32[128,16,128]{2,1,0:T(8,128)}, f32[128,16,128]{2,1,0:T(8,128)S(1)}, u32[]{:S(2)}, u32[]{:S(2)}) collective-permute-start(f32[128,16,128]{2,1,0:T(8,128)} %get-tuple-element.42), channel_id=1, source_target_pairs={{0,4},{4,0},{1,5},{5,1},{2,6},{6,2},{3,7},{7,3}} | collective-permute-start | bytes 3145736 | tf_op jit(solution)/shard_map/ppermute | solution.py:158
  150.4 115.1 %copy-start.3 = (f32[128,16,128]{2,1,0:T(8,128)S(1)}, f32[128,16,128]{2,1,0:T(8,128)}, u32[]{:S(2)}) copy-start(f32[128,16,128]{2,1,0:T(8,128)} %get-tuple-element.51) | copy-start | bytes 3145732
  150.5 115.3 %copy-start.2 = (f32[128,16,128]{2,1,0:T(8,128)S(1)}, f32[128,16,128]{2,1,0:T(8,128)}, u32[]{:S(2)}) copy-start(f32[128,16,128]{2,1,0:T(8,128)} %get-tuple-element.53) | copy-start | bytes 3145732
  150.5 143.6 %copy-start.5 = (f32[128,16,128]{2,1,0:T(8,128)S(1)}, f32[128,16,128]{2,1,0:T(8,128)}, u32[]{:S(2)}) copy-start(f32[128,16,128]{2,1,0:T(8,128)} %get-tuple-element.39) | copy-start | bytes 3145732
  150.5 22.7 %collective-permute-start.17 = (f32[128,16,128]{2,1,0:T(8,128)}, f32[128,16,128]{2,1,0:T(8,128)S(1)}, u32[]{:S(2)}, u32[]{:S(2)}) collective-permute-start(f32[128,16,128]{2,1,0:T(8,128)} %get-tuple-element.46), channel_id=1, source_target_pairs={{0,4},{4,0},{1,5},{5,1},{2,6},{6,2},{3,7},{7,3}} | collective-permute-start | bytes 3145736 | tf_op jit(solution)/shard_map/ppermute | solution.py:158
  151.2 44.4 %collective-permute-start.19 = (f32[128,16,128]{2,1,0:T(8,128)}, f32[128,16,128]{2,1,0:T(8,128)S(1)}, u32[]{:S(2)}, u32[]{:S(2)}) collective-permute-start(f32[128,16,128]{2,1,0:T(8,128)} %get-tuple-element.48), channel_id=1, source_target_pairs={{0,4},{4,0},{1,5},{5,1},{2,6},{6,2},{3,7},{7,3}} | collective-permute-start | bytes 3145736 | tf_op jit(solution)/shard_map/ppermute | solution.py:158
  152.5 65.6 %collective-permute-start.21 = (f32[128,16,128]{2,1,0:T(8,128)}, f32[128,16,128]{2,1,0:T(8,128)S(1)}, u32[]{:S(2)}, u32[]{:S(2)}) collective-permute-start(f32[128,16,128]{2,1,0:T(8,128)} %get-tuple-element.50), channel_id=1, source_target_pairs={{0,4},{4,0},{1,5},{5,1},{2,6},{6,2},{3,7},{7,3}} | collective-permute-start | bytes 3145736 | tf_op jit(solution)/shard_map/ppermute | solution.py:158
  153.3 87.4 %collective-permute-start.23 = (f32[128,16,128]{2,1,0:T(8,128)}, f32[128,16,128]{2,1,0:T(8,128)S(1)}, u32[]{:S(2)}, u32[]{:S(2)}) collective-permute-start(f32[128,16,128]{2,1,0:T(8,128)} %get-tuple-element.52), channel_id=1, source_target_pairs={{0,4},{4,0},{1,5},{5,1},{2,6},{6,2},{3,7},{7,3}} | collective-permute-start | bytes 3145736 | tf_op jit(solution)/shard_map/ppermute | solution.py:158
  154.6 108.5 %collective-permute-start.25 = (f32[128,16,128]{2,1,0:T(8,128)}, f32[128,16,128]{2,1,0:T(8,128)S(1)}, u32[]{:S(2)}, u32[]{:S(2)}) collective-permute-start(f32[128,16,128]{2,1,0:T(8,128)} %get-tuple-element.54), channel_id=1, source_target_pairs={{0,4},{4,0},{1,5},{5,1},{2,6},{6,2},{3,7},{7,3}} | collective-permute-start | bytes 3145736 | tf_op jit(solution)/shard_map/ppermute | solution.py:158
  155.4 158.0 %copy-start.6 = (f32[128,16,128]{2,1,0:T(8,128)S(1)}, f32[128,16,128]{2,1,0:T(8,128)}, u32[]{:S(2)}) copy-start(f32[128,16,128]{2,1,0:T(8,128)} %get-tuple-element.55) | copy-start | bytes 3145732
  173.2 112.4 %collective-permute-start.3 = (f32[128,16,128]{2,1,0:T(8,128)S(1)}, f32[128,16,128]{2,1,0:T(8,128)S(1)}, u32[]{:S(2)}, u32[]{:S(2)}) collective-permute-start(f32[128,16,128]{2,1,0:T(8,128)S(1)} %copy-done.13), channel_id=1, source_target_pairs={{0,4},{4,0},{1,5},{5,1},{2,6},{6,2},{3,7},{7,3}} | collective-permute-start | bytes 3145736 | tf_op jit(solution)/shard_map/ppermute | solution.py:158
  195.7 112.4 %collective-permute-start.27 = (f32[128,16,128]{2,1,0:T(8,128)}, f32[128,16,128]{2,1,0:T(8,128)S(1)}, u32[]{:S(2)}, u32[]{:S(2)}) collective-permute-start(f32[128,16,128]{2,1,0:T(8,128)} %get-tuple-element.56), channel_id=1, source_target_pairs={{0,4},{4,0},{1,5},{5,1},{2,6},{6,2},{3,7},{7,3}} | collective-permute-start | bytes 3145736 | tf_op jit(solution)/shard_map/ppermute | solution.py:158
  218.1 71.3 %collective-permute-start.5 = (bf16[128,16,128]{2,1,0:T(8,128)(2,1)S(1)}, bf16[128,16,128]{2,1,0:T(8,128)(2,1)S(1)}, u32[]{:S(2)}, u32[]{:S(2)}) collective-permute-start(bf16[128,16,128]{2,1,0:T(8,128)(2,1)S(1)} %add_convert_fusion.8), channel_id=1, source_target_pairs={{0,1},{1,0},{2,3},{3,2},{4,5},{5,4},{6,7},{7,6}} | collective-permute-start | bytes 1572872 | tf_op jit(solution)/shard_map/ppermute | solution.py:155
  240.6 53.5 %collective-permute-start.18 = (bf16[128,16,128]{2,1,0:T(8,128)(2,1)S(1)}, bf16[128,16,128]{2,1,0:T(8,128)(2,1)S(1)}, u32[]{:S(2)}, u32[]{:S(2)}) collective-permute-start(bf16[128,16,128]{2,1,0:T(8,128)(2,1)S(1)} %add_convert_fusion.7), channel_id=1, source_target_pairs={{0,2},{1,3},{2,0},{3,1},{4,6},{5,7},{6,4},{7,5}} | collective-permute-start | bytes 1572872 | tf_op jit(solution)/shard_map/ppermute | solution.py:155
  263.1 31.0 %collective-permute-start.20 = (bf16[128,16,128]{2,1,0:T(8,128)(2,1)S(1)}, bf16[128,16,128]{2,1,0:T(8,128)(2,1)S(1)}, u32[]{:S(2)}, u32[]{:S(2)}) collective-permute-start(bf16[128,16,128]{2,1,0:T(8,128)(2,1)S(1)} %add_convert_fusion.6), channel_id=1, source_target_pairs={{0,3},{1,2},{2,1},{3,0},{4,7},{5,6},{6,5},{7,4}} | collective-permute-start | bytes 1572872 | tf_op jit(solution)/shard_map/ppermute | solution.py:155
  285.6 22.5 %collective-permute-start.22 = (bf16[128,16,128]{2,1,0:T(8,128)(2,1)S(1)}, bf16[128,16,128]{2,1,0:T(8,128)(2,1)S(1)}, u32[]{:S(2)}, u32[]{:S(2)}) collective-permute-start(bf16[128,16,128]{2,1,0:T(8,128)(2,1)S(1)} %add_convert_fusion.4), channel_id=1, source_target_pairs={{0,2},{1,3},{2,0},{3,1},{4,6},{5,7},{6,4},{7,5}} | collective-permute-start | bytes 1572872 | tf_op jit(solution)/shard_map/ppermute | solution.py:155
  289.4 24.0 %collective-permute-start.24 = (bf16[128,16,128]{2,1,0:T(8,128)(2,1)S(1)}, bf16[128,16,128]{2,1,0:T(8,128)(2,1)S(1)}, u32[]{:S(2)}, u32[]{:S(2)}) collective-permute-start(bf16[128,16,128]{2,1,0:T(8,128)(2,1)S(1)} %add_convert_fusion.3), channel_id=1, source_target_pairs={{0,3},{1,2},{2,1},{3,0},{4,7},{5,6},{6,5},{7,4}} | collective-permute-start | bytes 1572872 | tf_op jit(solution)/shard_map/ppermute | solution.py:155
  294.1 19.3 %collective-permute-start.26 = (bf16[128,16,128]{2,1,0:T(8,128)(2,1)S(1)}, bf16[128,16,128]{2,1,0:T(8,128)(2,1)S(1)}, u32[]{:S(2)}, u32[]{:S(2)}) collective-permute-start(bf16[128,16,128]{2,1,0:T(8,128)(2,1)S(1)} %add_convert_fusion.2), channel_id=1, source_target_pairs={{0,1},{1,0},{2,3},{3,2},{4,5},{5,4},{6,7},{7,6}} | collective-permute-start | bytes 1572872 | tf_op jit(solution)/shard_map/ppermute | solution.py:155

commit v2 on v1

--- a/solution.py
+++ b/solution.py
@@ -13,7 +13,6 @@
 TILE = 256
 PAD = 16
 STEP = 16
-SLOTS = 2
 
 
 def share_kernel(n_grp, n_loc, mine_ref, all_ref, send_sem, recv_sem):
@@ -66,7 +65,7 @@
             acc[s] = v
 
 
-def pass_kernel(n_local, list_len, n_pad, row_block, x_places, out_places, cnt_ref, list_ref, gate_ref, *refs):
+def pass_kernel(n_slots, split, n_local, list_len, n_pad, row_block, x_places, out_places, cnt_ref, list_ref, gate_ref, *refs):
     n_x, n_out = len(x_places), len(out_places)
     stride = row_block + 4
     x_hbm, (wg_hbm, wu_hbm, wd_hbm), refs = refs[:n_x], refs[n_x:n_x + 3], refs[n_x + 3:]
@@ -83,7 +82,7 @@
     x_copies = [pltpu.make_async_copy(src, x_ref.at[pl.ds(at, src.shape[0])], x_sem.at[k]) for k, (src, at) in enumerate(zip(x_hbm, x_places))]
     for copy in x_copies:
         copy.start()
-    for e in range(SLOTS):
+    for e in range(n_slots):
         for copy in weights(e, e):
             copy.start()
     zero_acc(acc)
@@ -91,12 +90,14 @@
         copy.wait()
 
     def expert(e, carry):
-        slot = lax.rem(e, SLOTS)
+        slot = lax.rem(e, n_slots)
         n = cnt_ref[e]
         now = weights(e, slot)
-        now[0].wait()
-        now[1].wait()
-        now[2].wait()
+        ahead = weights(e + n_slots, slot)
+        n_blocks = jnp.maximum((n + row_block - 1) // row_block, 1)
+        if not split:
+            for copy in now:
+                copy.wait()
 
         def block(b, c):
             base = b * row_block
@@ -110,11 +111,29 @@
             lax.fori_loop(0, steps, gather, 0)
             for j in range(d_model // LANES):
                 xg[:, j * LANES:(j + 1) * LANES] = xs[pl.ds(j * stride, row_block), :].astype(jnp.bfloat16)
+
+            if split:
+                @pl.when(b == 0)
+                def _():
+                    now[0].wait()
+                    now[1].wait()
+
             for q in range(d_ff // TILE):
                 cols = slice(q * TILE, (q + 1) * TILE)
                 u = jnp.dot(xg[...], wg_ref[slot, :, cols], preferred_element_type=jnp.float32)
                 v = jnp.dot(xg[...], wu_ref[slot, :, cols], preferred_element_type=jnp.float32)
                 hid[:, cols] = (jax.nn.silu(u) * v).astype(jnp.bfloat16)
+
+            if split:
+                @pl.when(b == 0)
+                def _():
+                    now[2].wait()
+
+                @pl.when((b == n_blocks - 1) & (e + n_slots < n_local))
+                def _():
+                    ahead[0].start()
+                    ahead[1].start()
+
             for q in range(d_model // TILE):
                 o = jnp.dot(hid[...], wd_ref[slot, :, q * TILE:(q + 1) * TILE], preferred_element_type=jnp.float32)
                 for k in range(TILE // LANES):
@@ -127,11 +146,11 @@
             lax.fori_loop(0, steps, scatter, 0)
             return c
 
-        lax.fori_loop(0, (n + row_block - 1) // row_block, block, 0)
-
-        @pl.when(e + SLOTS < n_local)
+        lax.fori_loop(0, n_blocks, block, 0)
+
+        @pl.when(e + n_slots < n_local)
         def _():
-            for copy in weights(e + SLOTS, slot):
+            for copy in ahead[2:] if split else ahead:
                 copy.start()
 
         return carry
@@ -189,6 +208,7 @@
         y_low = swap_loc(low)
         c_low = swap_grp(low, 1)
         yc_low = swap_grp(y_low, 1)
+        c_high = swap_grp(high, 1)
         y_high = swap_loc(high)
         x_low = swap_grp(low, 2)
         x_high = swap_grp(high, 2)
@@ -197,7 +217,7 @@
         d_high = swap_diag(late)
         parts = {
             0: [low, high],
-            1: [c_low, swap_grp(high, 1)],
+            1: [c_low, c_high],
             2: [x_low, x_high],
             3: [swap_grp(x_low, 1), swap_grp(x_high, 1)],
             4: [y_low, y_high],
@@ -207,13 +227,16 @@
         }
 
         cube = meta_all.transpose(1, 0, 2).reshape(2 * top_k, 2, 2, 2, 2, mid)
-        near_meta = cube[:, :, 0, :, 0].reshape(2 * top_k, -1)
-        far_meta = jnp.concatenate([cube[:, :, 1].reshape(2 * top_k, 2, 4, mid), cube[:, :, 0, :, 1]], axis=2).reshape(2 * top_k, -1)
+        near_keep, near_send = [(0, 0), (0, 1), (1, 0), (1, 1), (2, 0), (3, 0)], [(4, 0), (5, 0)]
+        far_keep, far_send = [(2, 1), (3, 1)], [(4, 1), (5, 1), (6, 0), (6, 1), (7, 0), (7, 1)]
+
+        def join(*blocks):
+            return jnp.concatenate([b.reshape(2 * top_k, -1, mid) for b in blocks], axis=1).reshape(2 * top_k, -1)
+
         any_spec = pl.BlockSpec(memory_space=pl.ANY)
         piece = jax.ShapeDtypeStruct((mid, chunks, LANES), jnp.float32)
 
-        def run_pass(homes, meta, row_block, before=None):
-            blocks = [(k + dy * n_grp, h) for dy in range(n_loc) for k, h in homes]
+        def run_pass(blocks, meta, row_block, n_slots, split, before=None):
             n_rows = len(blocks) * mid
             n_pad = n_rows + PAD
             list_len = -(-min(capacity, n_rows) // row_block) * row_block
@@ -231,12 +254,12 @@
 
             x_parts = [parts[r][h] for r, h in blocks]
             x_places = [p * mid for p in range(len(blocks))]
-            out_places = x_places[len(homes):] + x_places[:len(homes)]
+            out_places = x_places
             stride = row_block + 4
             if before is not None:
                 count, before = lax.optimization_barrier((count, before))
             run = pl.pallas_call(
-                functools.partial(pass_kernel, n_local, list_len, n_pad, row_block, x_places, out_places),
+                functools.partial(pass_kernel, n_slots, split, n_local, list_len, n_pad, row_block, x_places, out_places),
                 grid_spec=pltpu.PrefetchScalarGridSpec(
                     num_scalar_prefetch=3,
                     grid=(),
@@ -248,11 +271,11 @@
                         pltpu.VMEM((chunks * stride, LANES), jnp.float32),
                         pltpu.VMEM((row_block, d_model), jnp.bfloat16),
                         pltpu.VMEM((row_block, d_ff), jnp.bfloat16),
-                        pltpu.VMEM((SLOTS, d_model, d_ff), jnp.bfloat16),
-                        pltpu.VMEM((SLOTS, d_model, d_ff), jnp.bfloat16),
-                        pltpu.VMEM((SLOTS, d_ff, d_model), jnp.bfloat16),
+                        pltpu.VMEM((n_slots, d_model, d_ff), jnp.bfloat16),
+                        pltpu.VMEM((n_slots, d_model, d_ff), jnp.bfloat16),
+                        pltpu.VMEM((n_slots, d_ff, d_model), jnp.bfloat16),
                         pltpu.SemaphoreType.DMA((len(x_parts),)),
-                        pltpu.SemaphoreType.DMA((SLOTS, 3)),
+                        pltpu.SemaphoreType.DMA((n_slots, 3)),
                         pltpu.SemaphoreType.DMA((len(out_places),)),
                     ],
                 ),
@@ -261,16 +284,14 @@
                 cost_estimate=pl.CostEstimate(flops=25 * 10**9, bytes_accessed=110 * 10**6, transcendentals=0),
             )
             outs = run(count, rows, gate_of, *x_parts, w_gate, w_up, w_down)
-            pieces = {home: (outs[i], outs[len(homes) + i]) for i, home in enumerate(homes)}
-            return {**(before or {}), **pieces}
-
-        near, far = [(0, 0), (1, 0)], [(2, 0), (2, 1), (3, 0), (3, 1), (0, 1), (1, 1)]
-        pieces = run_pass(near, near_meta, 96)
-        pieces = run_pass(far, far_meta, 208, pieces)
+            return {**(before or {}), **dict(zip(blocks, outs))}
+
+        pieces = run_pass(near_send + near_keep, join(cube[:, 1, 0, :, 0], cube[:, 0, 0], cube[:, 0, 1, :, 0]), 144, 3, True)
+        pieces = run_pass(far_send + far_keep, join(cube[:, 1, 0, :, 1], cube[:, 1, 1], cube[:, 0, 1, :, 1]), 144, 3, True, pieces)
 
         totals = [None, None]
-        for k, h in near + [(2, 0), (2, 1), (3, 0), (3, 1), (1, 1), (0, 1)]:
-            send, keep = pieces[k, h]
+        for k, h in [(0, 0), (1, 0), (2, 0), (2, 1), (3, 0), (3, 1), (1, 1), (0, 1)]:
+            send, keep = pieces[k + n_grp, h], pieces[k, h]
             mixed = (keep + swap_loc(send)).astype(jnp.bfloat16)
             back = (swap_grp(mixed, k) if k else mixed).astype(jnp.float32)
             totals[h] = back if totals[h] is None else totals[h] + back

time: 316 us -> 311 us (0.984)
  Pallas kernels: 95.4 us -> 88.9 us
    ppermute x16, waiting for transfers between devices: 5.45 us -> 13.6 us  [swap_grp(): return lax.ppermute(a, 'grp', [(i, i ^ bits) for i in range(n_grp)])]
    ppermute x11, waiting for transfers between devices: 151 us -> 144 us  [swap_loc(): return lax.ppermute(a, 'loc', [(i, i ^ 1) for i in range(n_loc)])]
    pallas_call x2, Pallas kernels: 86.9 us -> 80.4 us  [run_pass(): outs = run(count, rows, gate_of, *x_parts, w_gate, w_up, w_down)]
    another operation x7 -> x6, other arithmetic: 4.32 us -> 6.64 us
  transfers between devices with their start and end apart: 28 -> 28, of which waited for: 11 -> 12; matrix products, arithmetic and copies ran while one was open for 6% -> 7% of each run, Pallas kernels for 28% -> 26%
where the time goes in v2:
time: 311 us; the launch traced here: 310 us
  waiting for transfers between devices  157 us (50%)
  Pallas kernels  88.9 us (29%)
  starting transfers between devices  37.1 us (12%)
  other arithmetic  19.7 us (6%)
  local copies, waits for them, and re-layouts  6.53 us (2%)
    ppermute x11, waiting for transfers between devices, swap_loc(): return lax.ppermute(a, 'loc', [(i, i ^ 1) for i in range(n_loc)])  144 us
    pallas_call x2, Pallas kernels, run_pass(): outs = run(count, rows, gate_of, *x_parts, w_gate, w_up, w_down)  80.4 us
    ppermute x16, starting transfers between devices, swap_grp(): return lax.ppermute(a, 'grp', [(i, i ^ bits) for i in range(n_grp)])  26.8 us
    ppermute x16, waiting for transfers between devices, swap_grp(): return lax.ppermute(a, 'grp', [(i, i ^ bits) for i in range(n_grp)])  13.6 us
    ppermute x11, starting transfers between devices, swap_loc(): return lax.ppermute(a, 'loc', [(i, i ^ 1) for i in range(n_loc)])  8.74 us
    pallas_call x1, Pallas kernels, device_step(): pl.pallas_call(functools.partial(share_kernel, n_grp, n_loc), out_shape=j...  8.51 us
    another operation x6, other arithmetic  6.64 us
  transfers between devices with their start and end apart: 28, of which 12 were waited for; matrix products, arithmetic and copies ran while one was open for 7% of the time, Pallas kernels for 26%

profile of v2, /device:TPU:0, one launch (start us, length us, event | category | flops | bytes accessed | tf_op | source)
XLA Modules:
  0.0 309.9 jit_solution(17420856912649900632)
XLA Ops:
  0.0 0.7 convert_bitcast_fusion.2
  0.7 1.3 pad_maximum_fusion.3.mine_ref
  2.0 8.5 %share.1 = f32[8,16,256]{2,1,0:T(8,128)} custom-call(f32[16,256]{1,0:T(8,128)} %pad_maximum_fusion.3.mine_ref), custom_call_target="tpu_custom_call" | custom-call | tf_op jit(solution)/shard_map/share/pallas_call | solution.py:195
  10.5 1.3 slice_bitcast_fusion
  11.8 0.1 copy.38
  12.1 1.5 collective-permute-start.4
  13.6 1.5 collective-permute-start
  15.1 0.6 collective-permute-start.15
  15.6 0.5 collective-permute-start.9
  16.2 1.0 reshape.126
  17.3 0.2 compare_reduce_fusion
  17.6 2.3 reduce-window.16
  19.8 0.3 slice_reduce_fusion
  20.1 0.2 reduce-window.19
  20.4 2.3 reduce-window.14
  22.7 0.3 slice_reduce_fusion.1
  22.9 0.2 reduce-window.15
  23.2 0.2 fusion
  23.4 0.7 reshape.130.gate_ref
  24.1 0.7 reshape.129.gate_ref
  25.2 2.4 convert_reduce_fusion.1
  27.6 0.8 collective-permute-done.refs_0_
  28.4 1.6 collective-permute-start.12
  30.1 0.6 collective-permute-start.11
  30.6 7.5 %collective-permute-done.15.refs_6_ = bf16[128,16,128]{2,1,0:T(8,128)(2,1)S(1)} collective-permute-done((bf16[128,16,128]{2,1,0:T(8,128)(2,1)S(1)}, bf16[128,16,128]{2,1,0:T(8,128)(2,1)S(1)}, u32[]{:S(2)}, u32[]{:S(2)}) %collective-permute-start.15) | collective-permute-done | bytes 524320 | tf_op jit(solution)/shard_map/ppermute | solution.py:174
  38.1 12.8 %collective-permute-done.9.refs_0_ = bf16[128,16,128]{2,1,0:T(8,128)(2,1)} collective-permute-done((bf16[128,16,128]{2,1,0:T(8,128)(2,1)S(1)}, bf16[128,16,128]{2,1,0:T(8,128)(2,1)}, u32[]{:S(2)}, u32[]{:S(2)}) %collective-permute-start.9) | collective-permute-done | bytes 524320 | tf_op jit(solution)/shard_map/ppermute | solution.py:177
  51.0 2.4 convert_reduce_fusion
  53.4 0.7 select_n.43.list_ref
  54.1 0.7 select_n.40.list_ref
  54.8 0.5 collective-permute-start.16
  55.3 6.4 %collective-permute-done.11.refs_2_ = bf16[128,16,128]{2,1,0:T(8,128)(2,1)} collective-permute-done((bf16[128,16,128]{2,1,0:T(8,128)(2,1)S(1)}, bf16[128,16,128]{2,1,0:T(8,128)(2,1)}, u32[]{:S(2)}, u32[]{:S(2)}) %collective-permute-start.11) | collective-permute-done | bytes 524320 | tf_op jit(solution)/shard_map/ppermute | solution.py:177
  61.7 0.5 collective-permute-start.13
  62.3 40.1 %shard_map.64 = (f32[128,16,128]{2,1,0:T(8,128)}, f32[128,16,128]{2,1,0:T(8,128)}, f32[128,16,128]{2,1,0:T(8,128)}, f32[128,16,128]{2,1,0:T(8,128)}, f32[128,16,...) custom-call(s32[8]{0:T(128)} %bitcast.90, ...), custom_call_target="tpu_custom_call" | custom-call | flops 24999999488 | bytes 110000000 | tf_op jit(solution)/shard_map/pallas_call | solution.py:286
  102.5 1.6 collective-permute-start.7
  104.1 40.3 %shard_map.65 = (f32[128,16,128]{2,1,0:T(8,128)}, f32[128,16,128]{2,1,0:T(8,128)}, f32[128,16,128]{2,1,0:T(8,128)}, f32[128,16,128]{2,1,0:T(8,128)}, f32[128,16,...) custom-call(s32[8]{0:T(128)} %bitcast.88, ...), custom_call_target="tpu_custom_call" | custom-call | flops 24999999488 | bytes 110000000 | tf_op jit(solution)/shard_map/pallas_call | solution.py:286
  144.4 0.5 collective-permute-start.17
  145.0 1.5 collective-permute-start.19
  146.5 0.5 collective-permute-start.21
  147.0 1.5 collective-permute-start.23
  148.5 0.5 collective-permute-start.25
  149.0 1.4 add_convert_fusion.8
  150.4 17.1 %collective-permute-done.17 = f32[128,16,128]{2,1,0:T(8,128)S(1)} collective-permute-done((f32[128,16,128]{2,1,0:T(8,128)}, f32[128,16,128]{2,1,0:T(8,128)S(1)}, u32[]{:S(2)}, u32[]{:S(2)}) %collective-permute-start.17) | collective-permute-done | bytes 1048608 | tf_op jit(solution)/shard_map/ppermute | solution.py:177
  167.6 0.1 add_convert_fusion.7
  167.7 22.3 %collective-permute-done.19 = f32[128,16,128]{2,1,0:T(8,128)S(1)} collective-permute-done((f32[128,16,128]{2,1,0:T(8,128)}, f32[128,16,128]{2,1,0:T(8,128)S(1)}, u32[]{:S(2)}, u32[]{:S(2)}) %collective-permute-start.19) | collective-permute-done | bytes 1048608 | tf_op jit(solution)/shard_map/ppermute | solution.py:177
  190.0 0.1 add_convert_fusion.6
  190.2 22.3 %collective-permute-done.21 = f32[128,16,128]{2,1,0:T(8,128)S(1)} collective-permute-done((f32[128,16,128]{2,1,0:T(8,128)}, f32[128,16,128]{2,1,0:T(8,128)S(1)}, u32[]{:S(2)}, u32[]{:S(2)}) %collective-permute-start.21) | collective-permute-done | bytes 1048608 | tf_op jit(solution)/shard_map/ppermute | solution.py:177
  212.5 6.4 %collective-permute-start.8 = (bf16[128,16,128]{2,1,0:T(8,128)(2,1)S(1)}, bf16[128,16,128]{2,1,0:T(8,128)(2,1)S(1)}, u32[]{:S(2)}, u32[]{:S(2)}) collective-permute-start(bf16[128,16,128]{2,1,0:T(8,128)(2,1)S(1)} %add_convert_fusion.8), channel_id=1, source_target_pairs={{0,1},{1,0},{2,3},{3,2},{4,5},{5,4},{6,7},{7,6}} | collective-permute-start | bytes 1572872 | tf_op jit(solution)/shard_map/ppermute | solution.py:174
  218.9 1.4 add_convert_fusion.4
  220.3 14.7 %collective-permute-done.23 = f32[128,16,128]{2,1,0:T(8,128)S(1)} collective-permute-done((f32[128,16,128]{2,1,0:T(8,128)}, f32[128,16,128]{2,1,0:T(8,128)S(1)}, u32[]{:S(2)}, u32[]{:S(2)}) %collective-permute-start.23) | collective-permute-done | bytes 1048608 | tf_op jit(solution)/shard_map/ppermute | solution.py:177
  235.0 4.5 %collective-permute-start.18 = (bf16[128,16,128]{2,1,0:T(8,128)(2,1)S(1)}, bf16[128,16,128]{2,1,0:T(8,128)(2,1)S(1)}, u32[]{:S(2)}, u32[]{:S(2)}) collective-permute-start(bf16[128,16,128]{2,1,0:T(8,128)(2,1)S(1)} %add_convert_fusion.7), channel_id=1, source_target_pairs={{0,2},{1,3},{2,0},{3,1},{4,6},{5,7},{6,4},{7,5}} | collective-permute-start | bytes 1572872 | tf_op jit(solution)/shard_map/ppermute | solution.py:174
  239.4 18.0 %collective-permute-done.25 = f32[128,16,128]{2,1,0:T(8,128)S(1)} collective-permute-done((f32[128,16,128]{2,1,0:T(8,128)}, f32[128,16,128]{2,1,0:T(8,128)S(1)}, u32[]{:S(2)}, u32[]{:S(2)}) %collective-permute-start.25) | collective-permute-done | bytes 1048608 | tf_op jit(solution)/shard_map/ppermute | solution.py:177
  257.4 5.0 %collective-permute-start.20 = (bf16[128,16,128]{2,1,0:T(8,128)(2,1)S(1)}, bf16[128,16,128]{2,1,0:T(8,128)(2,1)S(1)}, u32[]{:S(2)}, u32[]{:S(2)}) collective-permute-start(bf16[128,16,128]{2,1,0:T(8,128)(2,1)S(1)} %add_convert_fusion.6), channel_id=1, source_target_pairs={{0,3},{1,2},{2,1},{3,0},{4,7},{5,6},{6,5},{7,4}} | collective-permute-start | bytes 1572872 | tf_op jit(solution)/shard_map/ppermute | solution.py:174
  262.4 1.4 add_convert_fusion.3
  263.8 0.1 add_convert_fusion.2
  263.9 16.0 %collective-permute-done.6 = f32[128,16,128]{2,1,0:T(8,128)S(1)} collective-permute-done((f32[128,16,128]{2,1,0:T(8,128)}, f32[128,16,128]{2,1,0:T(8,128)S(1)}, u32[]{:S(2)}, u32[]{:S(2)}) %collective-permute-start.6) | collective-permute-done | bytes 1048608 | tf_op jit(solution)/shard_map/ppermute | solution.py:177
  279.9 4.5 %collective-permute-start.22 = (bf16[128,16,128]{2,1,0:T(8,128)(2,1)S(1)}, bf16[128,16,128]{2,1,0:T(8,128)(2,1)S(1)}, u32[]{:S(2)}, u32[]{:S(2)}) collective-permute-start(bf16[128,16,128]{2,1,0:T(8,128)(2,1)S(1)} %add_convert_fusion.4), channel_id=1, source_target_pairs={{0,2},{1,3},{2,0},{3,1},{4,6},{5,7},{6,4},{7,5}} | collective-permute-start | bytes 1572872 | tf_op jit(solution)/shard_map/ppermute | solution.py:174
  284.4 3.3 %collective-permute-start.24 = (bf16[128,16,128]{2,1,0:T(8,128)(2,1)S(1)}, bf16[128,16,128]{2,1,0:T(8,128)(2,1)S(1)}, u32[]{:S(2)}, u32[]{:S(2)}) collective-permute-start(bf16[128,16,128]{2,1,0:T(8,128)(2,1)S(1)} %add_convert_fusion.3), channel_id=1, source_target_pairs={{0,3},{1,2},{2,1},{3,0},{4,7},{5,6},{6,5},{7,4}} | collective-permute-start | bytes 1572872 | tf_op jit(solution)/shard_map/ppermute | solution.py:174
  287.7 1.5 add_convert_fusion.5
  289.2 0.1 copy.48
  289.3 13.0 %collective-permute-done.27 = f32[128,16,128]{2,1,0:T(8,128)S(1)} collective-permute-done((f32[128,16,128]{2,1,0:T(8,128)}, f32[128,16,128]{2,1,0:T(8,128)S(1)}, u32[]{:S(2)}, u32[]{:S(2)}) %collective-permute-start.27) | collective-permute-done | bytes 1048608 | tf_op jit(solution)/shard_map/ppermute | solution.py:177
  302.4 6.0 %collective-permute-done.24 = bf16[128,16,128]{2,1,0:T(8,128)(2,1)S(1)} collective-permute-done((bf16[128,16,128]{2,1,0:T(8,128)(2,1)S(1)}, bf16[128,16,128]{2,1,0:T(8,128)(2,1)S(1)}, u32[]{:S(2)}, u32[]{:S(2)}) %collective-permute-start.24) | collective-permute-done | bytes 524320 | tf_op jit(solution)/shard_map/ppermute | solution.py:174
  308.4 0.3 add_convert_fusion
  308.7 0.1 copy.47
  308.8 1.1 pad_maximum_fusion
  (76 shorter events, 1.0 us)
Async XLA Ops:
  11.9 50.4 %copy-start = (bf16[16,8,16,128]{3,2,1,0:T(8,128)(2,1)}, bf16[16,8,16,128]{3,2,1,0:T(8,128)(2,1)S(1)}, u32[]{:S(2)}) copy-start(bf16[16,8,16,128]{3,2,1,0:T(8,128)(2,1)S(1)} %copy.38) | copy-start | bytes 1572868
  12.1 50.2 %copy-start.1 = (bf16[16,8,16,128]{3,2,1,0:T(8,128)(2,1)}, bf16[16,8,16,128]{3,2,1,0:T(8,128)(2,1)S(1)}, u32[]{:S(2)}) copy-start(bf16[16,8,16,128]{3,2,1,0:T(8,128)(2,1)S(1)} %copy.37) | copy-start | bytes 1572868
  12.1 16.3 %collective-permute-start.4 = (bf16[128,16,128]{2,1,0:T(8,128)(2,1)S(1)}, bf16[128,16,128]{2,1,0:T(8,128)(2,1)S(1)}, u32[]{:S(2)}, u32[]{:S(2)}) collective-permute-start(bf16[128,16,128]{2,1,0:T(8,128)(2,1)S(1)} %bitcast.65), channel_id=1, source_target_pairs={{0,2},{1,3},{2,0},{3,1},{4,6},{5,7},{6,4},{7,5}} | collective-permute-start | bytes 1572872 | tf_op jit(solution)/shard_map/ppermute | solution.py:174
  13.6 16.5 %collective-permute-start.2 = (bf16[128,16,128]{2,1,0:T(8,128)(2,1)S(1)}, bf16[128,16,128]{2,1,0:T(8,128)(2,1)S(1)}, u32[]{:S(2)}, u32[]{:S(2)}) collective-permute-start(bf16[128,16,128]{2,1,0:T(8,128)(2,1)S(1)} %bitcast.66), channel_id=1, source_target_pairs={{0,1},{1,0},{2,3},{3,2},{4,5},{5,4},{6,7},{7,6}} | collective-permute-start | bytes 1572872 | tf_op jit(solution)/shard_map/ppermute | solution.py:174
  13.6 14.8 %collective-permute-start = (bf16[128,16,128]{2,1,0:T(8,128)(2,1)S(1)}, bf16[128,16,128]{2,1,0:T(8,128)(2,1)S(1)}, u32[]{:S(2)}, u32[]{:S(2)}) collective-permute-start(bf16[128,16,128]{2,1,0:T(8,128)(2,1)S(1)} %bitcast.67), channel_id=1, source_target_pairs={{0,4},{4,0},{1,5},{5,1},{2,6},{6,2},{3,7},{7,3}} | collective-permute-start | bytes 1572872 | tf_op jit(solution)/shard_map/ppermute | solution.py:177
  15.1 23.1 %collective-permute-start.15 = (bf16[128,16,128]{2,1,0:T(8,128)(2,1)S(1)}, bf16[128,16,128]{2,1,0:T(8,128)(2,1)S(1)}, u32[]{:S(2)}, u32[]{:S(2)}) collective-permute-start(bf16[128,16,128]{2,1,0:T(8,128)(2,1)S(1)} %bitcast.60), channel_id=1, source_target_pairs={{0,2},{1,3},{2,0},{3,1},{4,6},{5,7},{6,4},{7,5}} | collective-permute-start | bytes 1572872 | tf_op jit(solution)/shard_map/ppermute | solution.py:174
  15.6 35.3 %collective-permute-start.9 = (bf16[128,16,128]{2,1,0:T(8,128)(2,1)S(1)}, bf16[128,16,128]{2,1,0:T(8,128)(2,1)}, u32[]{:S(2)}, u32[]{:S(2)}) collective-permute-start(bf16[128,16,128]{2,1,0:T(8,128)(2,1)S(1)} %bitcast.61), channel_id=1, source_target_pairs={{0,4},{4,0},{1,5},{5,1},{2,6},{6,2},{3,7},{7,3}} | collective-permute-start | bytes 1572872 | tf_op jit(solution)/shard_map/ppermute | solution.py:177
  25.0 37.3 %copy-start.12 = (s32[8,1]{0,1:T(1,128)}, s32[8,1]{0,1:T(1,128)S(1)}, u32[]{:S(2)}) copy-start(s32[8,1]{0,1:T(1,128)S(1)} %copy.36) | copy-start | bytes 100
  25.2 77.3 %copy-start.11 = (s32[8,1]{0,1:T(1,128)}, s32[8,1]{0,1:T(1,128)S(1)}, u32[]{:S(2)}) copy-start(s32[8,1]{0,1:T(1,128)S(1)} %copy.32) | copy-start | bytes 100
  28.4 33.9 %copy-start.10 = (bf16[128,16,128]{2,1,0:T(8,128)(2,1)}, bf16[128,16,128]{2,1,0:T(8,128)(2,1)S(1)}, u32[]{:S(2)}) copy-start(bf16[128,16,128]{2,1,0:T(8,128)(2,1)S(1)} %collective-permute-done.refs_0_) | copy-start | bytes 1572868
  28.4 26.4 %collective-permute-start.3 = (bf16[128,16,128]{2,1,0:T(8,128)(2,1)S(1)}, bf16[128,16,128]{2,1,0:T(8,128)(2,1)}, u32[]{:S(2)}, u32[]{:S(2)}) collective-permute-start(bf16[128,16,128]{2,1,0:T(8,128)(2,1)S(1)} %bitcast.62), channel_id=1, source_target_pairs={{0,1},{1,0},{2,3},{3,2},{4,5},{5,4},{6,7},{7,6}} | collective-permute-start | bytes 1572872 | tf_op jit(solution)/shard_map/ppermute | solution.py:174
  28.4 33.9 %copy-start.8 = (bf16[128,16,128]{2,1,0:T(8,128)(2,1)}, bf16[128,16,128]{2,1,0:T(8,128)(2,1)S(1)}, u32[]{:S(2)}) copy-start(bf16[128,16,128]{2,1,0:T(8,128)(2,1)S(1)} %collective-permute-done.4.refs_6_) | copy-start | bytes 1572868
  28.4 33.8 %collective-permute-start.12 = (bf16[128,16,128]{2,1,0:T(8,128)(2,1)S(1)}, bf16[128,16,128]{2,1,0:T(8,128)(2,1)}, u32[]{:S(2)}, u32[]{:S(2)}) collective-permute-start(bf16[128,16,128]{2,1,0:T(8,128)(2,1)S(1)} %bitcast.63), channel_id=1, source_target_pairs={{0,6},{1,7},{2,4},{3,5},{4,2},{5,3},{6,0},{7,1}} | collective-permute-start | bytes 1572872 | tf_op jit(solution)/shard_map/ppermute | solution.py:181
  30.1 32.3 %copy-start.9 = (bf16[128,16,128]{2,1,0:T(8,128)(2,1)}, bf16[128,16,128]{2,1,0:T(8,128)(2,1)S(1)}, u32[]{:S(2)}) copy-start(bf16[128,16,128]{2,1,0:T(8,128)(2,1)S(1)} %collective-permute-done.2.refs_4_) | copy-start | bytes 1572868
  30.1 31.7 %collective-permute-start.11 = (bf16[128,16,128]{2,1,0:T(8,128)(2,1)S(1)}, bf16[128,16,128]{2,1,0:T(8,128)(2,1)}, u32[]{:S(2)}, u32[]{:S(2)}) collective-permute-start(bf16[128,16,128]{2,1,0:T(8,128)(2,1)S(1)} %collective-permute-done.4.refs_6_), channel_id=1, source_target_pairs={{0,4},{4,0},{1,5},{5,1},{2,6},{6,2},{3,7},{7,3}} | collective-permute-start | bytes 1572872 | tf_op jit(solution)/shard_map/ppermute | solution.py:177
  38.1 64.4 %copy-start.7 = (bf16[128,16,128]{2,1,0:T(8,128)(2,1)}, bf16[128,16,128]{2,1,0:T(8,128)(2,1)S(1)}, u32[]{:S(2)}) copy-start(bf16[128,16,128]{2,1,0:T(8,128)(2,1)S(1)} %collective-permute-done.15.refs_6_) | copy-start | bytes 1572868
  38.1 23.6 %collective-permute-start.5 = (bf16[128,16,128]{2,1,0:T(8,128)(2,1)S(1)}, bf16[128,16,128]{2,1,0:T(8,128)(2,1)}, u32[]{:S(2)}, u32[]{:S(2)}) collective-permute-start(bf16[128,16,128]{2,1,0:T(8,128)(2,1)S(1)} %collective-permute-done.4.refs_6_), channel_id=1, source_target_pairs={{0,1},{1,0},{2,3},{3,2},{4,5},{5,4},{6,7},{7,6}} | collective-permute-start | bytes 1572872 | tf_op jit(solution)/shard_map/ppermute | solution.py:174
  51.0 11.3 %collective-permute-start.1 = (bf16[128,16,128]{2,1,0:T(8,128)(2,1)S(1)}, bf16[128,16,128]{2,1,0:T(8,128)(2,1)}, u32[]{:S(2)}, u32[]{:S(2)}) collective-permute-start(bf16[128,16,128]{2,1,0:T(8,128)(2,1)S(1)} %collective-permute-done.refs_0_), channel_id=1, source_target_pairs={{0,1},{1,0},{2,3},{3,2},{4,5},{5,4},{6,7},{7,6}} | collective-permute-start | bytes 1572872 | tf_op jit(solution)/shard_map/ppermute | solution.py:174
  54.8 49.3 %collective-permute-start.16 = (bf16[128,16,128]{2,1,0:T(8,128)(2,1)S(1)}, bf16[128,16,128]{2,1,0:T(8,128)(2,1)}, u32[]{:S(2)}, u32[]{:S(2)}) collective-permute-start(bf16[128,16,128]{2,1,0:T(8,128)(2,1)S(1)} %collective-permute-done.15.refs_6_), channel_id=1, source_target_pairs={{0,1},{1,0},{2,3},{3,2},{4,5},{5,4},{6,7},{7,6}} | collective-permute-start | bytes 1572872 | tf_op jit(solution)/shard_map/ppermute | solution.py:174
  61.7 42.4 %collective-permute-start.10 = (bf16[128,16,128]{2,1,0:T(8,128)(2,1)}, bf16[128,16,128]{2,1,0:T(8,128)(2,1)}, u32[]{:S(2)}, u32[]{:S(2)}) collective-permute-start(bf16[128,16,128]{2,1,0:T(8,128)(2,1)} %collective-permute-done.9.refs_0_), channel_id=1, source_target_pairs={{0,1},{1,0},{2,3},{3,2},{4,5},{5,4},{6,7},{7,6}} | collective-permute-start | bytes 1572872 | tf_op jit(solution)/shard_map/ppermute | solution.py:174
  61.7 42.4 %collective-permute-start.13 = (bf16[128,16,128]{2,1,0:T(8,128)(2,1)}, bf16[128,16,128]{2,1,0:T(8,128)(2,1)}, u32[]{:S(2)}, u32[]{:S(2)}) collective-permute-start(bf16[128,16,128]{2,1,0:T(8,128)(2,1)} %collective-permute-done.11.refs_2_), channel_id=1, source_target_pairs={{0,1},{1,0},{2,3},{3,2},{4,5},{5,4},{6,7},{7,6}} | collective-permute-start | bytes 1572872 | tf_op jit(solution)/shard_map/ppermute | solution.py:174
  62.3 41.9 %collective-permute-start.14 = (bf16[128,16,128]{2,1,0:T(8,128)(2,1)}, bf16[128,16,128]{2,1,0:T(8,128)(2,1)}, u32[]{:S(2)}, u32[]{:S(2)}) collective-permute-start(bf16[128,16,128]{2,1,0:T(8,128)(2,1)} %collective-permute-done.12.refs_3_), channel_id=1, source_target_pairs={{0,1},{1,0},{2,3},{3,2},{4,5},{5,4},{6,7},{7,6}} | collective-permute-start | bytes 1572872 | tf_op jit(solution)/shard_map/ppermute | solution.py:174
  102.5 46.5 %copy-start.5 = (f32[128,16,128]{2,1,0:T(8,128)S(1)}, f32[128,16,128]{2,1,0:T(8,128)}, u32[]{:S(2)}) copy-start(f32[128,16,128]{2,1,0:T(8,128)} %get-tuple-element.49) | copy-start | bytes 3145732
  102.5 65.1 %copy-start.4 = (f32[128,16,128]{2,1,0:T(8,128)S(1)}, f32[128,16,128]{2,1,0:T(8,128)}, u32[]{:S(2)}) copy-start(f32[128,16,128]{2,1,0:T(8,128)} %get-tuple-element.51) | copy-start | bytes 3145732
  102.5 87.5 %copy-start.3 = (f32[128,16,128]{2,1,0:T(8,128)S(1)}, f32[128,16,128]{2,1,0:T(8,128)}, u32[]{:S(2)}) copy-start(f32[128,16,128]{2,1,0:T(8,128)} %get-tuple-element.55) | copy-start | bytes 3145732
  102.5 161.3 %copy-start.2 = (f32[128,16,128]{2,1,0:T(8,128)S(1)}, f32[128,16,128]{2,1,0:T(8,128)}, u32[]{:S(2)}) copy-start(f32[128,16,128]{2,1,0:T(8,128)} %get-tuple-element.61) | copy-start | bytes 3145732
  102.5 46.0 %collective-permute-start.7 = (f32[128,16,128]{2,1,0:T(8,128)}, f32[128,16,128]{2,1,0:T(8,128)}, u32[]{:S(2)}, u32[]{:S(2)}) collective-permute-start(f32[128,16,128]{2,1,0:T(8,128)} %get-tuple-element.50), channel_id=1, source_target_pairs={{0,4},{4,0},{1,5},{5,1},{2,6},{6,2},{3,7},{7,3}} | collective-permute-start | bytes 3145736 | tf_op jit(solution)/shard_map/ppermute | solution.py:177
  144.4 164.0 %copy-start.6 = (f32[128,16,128]{2,1,0:T(8,128)S(1)}, f32[128,16,128]{2,1,0:T(8,128)}, u32[]{:S(2)}) copy-start(f32[128,16,128]{2,1,0:T(8,128)} %get-tuple-element.63) | copy-start | bytes 3145732
  144.4 23.1 %collective-permute-start.17 = (f32[128,16,128]{2,1,0:T(8,128)}, f32[128,16,128]{2,1,0:T(8,128)S(1)}, u32[]{:S(2)}, u32[]{:S(2)}) collective-permute-start(f32[128,16,128]{2,1,0:T(8,128)} %get-tuple-element.54), channel_id=1, source_target_pairs={{0,4},{4,0},{1,5},{5,1},{2,6},{6,2},{3,7},{7,3}} | collective-permute-start | bytes 3145736 | tf_op jit(solution)/shard_map/ppermute | solution.py:177
  145.0 45.0 %collective-permute-start.19 = (f32[128,16,128]{2,1,0:T(8,128)}, f32[128,16,128]{2,1,0:T(8,128)S(1)}, u32[]{:S(2)}, u32[]{:S(2)}) collective-permute-start(f32[128,16,128]{2,1,0:T(8,128)} %get-tuple-element.56), channel_id=1, source_target_pairs={{0,4},{4,0},{1,5},{5,1},{2,6},{6,2},{3,7},{7,3}} | collective-permute-start | bytes 3145736 | tf_op jit(solution)/shard_map/ppermute | solution.py:177
  146.5 66.0 %collective-permute-start.21 = (f32[128,16,128]{2,1,0:T(8,128)}, f32[128,16,128]{2,1,0:T(8,128)S(1)}, u32[]{:S(2)}, u32[]{:S(2)}) collective-permute-start(f32[128,16,128]{2,1,0:T(8,128)} %get-tuple-element.58), channel_id=1, source_target_pairs={{0,4},{4,0},{1,5},{5,1},{2,6},{6,2},{3,7},{7,3}} | collective-permute-start | bytes 3145736 | tf_op jit(solution)/shard_map/ppermute | solution.py:177
  147.0 88.0 %collective-permute-start.23 = (f32[128,16,128]{2,1,0:T(8,128)}, f32[128,16,128]{2,1,0:T(8,128)S(1)}, u32[]{:S(2)}, u32[]{:S(2)}) collective-permute-start(f32[128,16,128]{2,1,0:T(8,128)} %get-tuple-element.60), channel_id=1, source_target_pairs={{0,4},{4,0},{1,5},{5,1},{2,6},{6,2},{3,7},{7,3}} | collective-permute-start | bytes 3145736 | tf_op jit(solution)/shard_map/ppermute | solution.py:177
  148.5 108.9 %collective-permute-start.25 = (f32[128,16,128]{2,1,0:T(8,128)}, f32[128,16,128]{2,1,0:T(8,128)S(1)}, u32[]{:S(2)}, u32[]{:S(2)}) collective-permute-start(f32[128,16,128]{2,1,0:T(8,128)} %get-tuple-element.62), channel_id=1, source_target_pairs={{0,4},{4,0},{1,5},{5,1},{2,6},{6,2},{3,7},{7,3}} | collective-permute-start | bytes 3145736 | tf_op jit(solution)/shard_map/ppermute | solution.py:177
  167.6 112.4 %collective-permute-start.6 = (f32[128,16,128]{2,1,0:T(8,128)}, f32[128,16,128]{2,1,0:T(8,128)S(1)}, u32[]{:S(2)}, u32[]{:S(2)}) collective-permute-start(f32[128,16,128]{2,1,0:T(8,128)} %get-tuple-element.48), channel_id=1, source_target_pairs={{0,4},{4,0},{1,5},{5,1},{2,6},{6,2},{3,7},{7,3}} | collective-permute-start | bytes 3145736 | tf_op jit(solution)/shard_map/ppermute | solution.py:177
  190.0 112.4 %collective-permute-start.27 = (f32[128,16,128]{2,1,0:T(8,128)}, f32[128,16,128]{2,1,0:T(8,128)S(1)}, u32[]{:S(2)}, u32[]{:S(2)}) collective-permute-start(f32[128,16,128]{2,1,0:T(8,128)} %get-tuple-element.64), channel_id=1, source_target_pairs={{0,4},{4,0},{1,5},{5,1},{2,6},{6,2},{3,7},{7,3}} | collective-permute-start | bytes 3145736 | tf_op jit(solution)/shard_map/ppermute | solution.py:177
  212.5 71.9 %collective-permute-start.8 = (bf16[128,16,128]{2,1,0:T(8,128)(2,1)S(1)}, bf16[128,16,128]{2,1,0:T(8,128)(2,1)S(1)}, u32[]{:S(2)}, u32[]{:S(2)}) collective-permute-start(bf16[128,16,128]{2,1,0:T(8,128)(2,1)S(1)} %add_convert_fusion.8), channel_id=1, source_target_pairs={{0,1},{1,0},{2,3},{3,2},{4,5},{5,4},{6,7},{7,6}} | collective-permute-start | bytes 1572872 | tf_op jit(solution)/shard_map/ppermute | solution.py:174
  235.0 52.7 %collective-permute-start.18 = (bf16[128,16,128]{2,1,0:T(8,128)(2,1)S(1)}, bf16[128,16,128]{2,1,0:T(8,128)(2,1)S(1)}, u32[]{:S(2)}, u32[]{:S(2)}) collective-permute-start(bf16[128,16,128]{2,1,0:T(8,128)(2,1)S(1)} %add_convert_fusion.7), channel_id=1, source_target_pairs={{0,2},{1,3},{2,0},{3,1},{4,6},{5,7},{6,4},{7,5}} | collective-permute-start | bytes 1572872 | tf_op jit(solution)/shard_map/ppermute | solution.py:174
  257.4 30.2 %collective-permute-start.20 = (bf16[128,16,128]{2,1,0:T(8,128)(2,1)S(1)}, bf16[128,16,128]{2,1,0:T(8,128)(2,1)S(1)}, u32[]{:S(2)}, u32[]{:S(2)}) collective-permute-start(bf16[128,16,128]{2,1,0:T(8,128)(2,1)S(1)} %add_convert_fusion.6), channel_id=1, source_target_pairs={{0,3},{1,2},{2,1},{3,0},{4,7},{5,6},{6,5},{7,4}} | collective-permute-start | bytes 1572872 | tf_op jit(solution)/shard_map/ppermute | solution.py:174
  279.9 22.5 %collective-permute-start.22 = (bf16[128,16,128]{2,1,0:T(8,128)(2,1)S(1)}, bf16[128,16,128]{2,1,0:T(8,128)(2,1)S(1)}, u32[]{:S(2)}, u32[]{:S(2)}) collective-permute-start(bf16[128,16,128]{2,1,0:T(8,128)(2,1)S(1)} %add_convert_fusion.4), channel_id=1, source_target_pairs={{0,2},{1,3},{2,0},{3,1},{4,6},{5,7},{6,4},{7,5}} | collective-permute-start | bytes 1572872 | tf_op jit(solution)/shard_map/ppermute | solution.py:174
  284.4 24.0 %collective-permute-start.24 = (bf16[128,16,128]{2,1,0:T(8,128)(2,1)S(1)}, bf16[128,16,128]{2,1,0:T(8,128)(2,1)S(1)}, u32[]{:S(2)}, u32[]{:S(2)}) collective-permute-start(bf16[128,16,128]{2,1,0:T(8,128)(2,1)S(1)} %add_convert_fusion.3), channel_id=1, source_target_pairs={{0,3},{1,2},{2,1},{3,0},{4,7},{5,6},{6,5},{7,4}} | collective-permute-start | bytes 1572872 | tf_op jit(solution)/shard_map/ppermute | solution.py:174
  287.7 20.7 %collective-permute-start.26 = (bf16[128,16,128]{2,1,0:T(8,128)(2,1)S(1)}, bf16[128,16,128]{2,1,0:T(8,128)(2,1)S(1)}, u32[]{:S(2)}, u32[]{:S(2)}) collective-permute-start(bf16[128,16,128]{2,1,0:T(8,128)(2,1)S(1)} %add_convert_fusion.2), channel_id=1, source_target_pairs={{0,1},{1,0},{2,3},{3,2},{4,5},{5,4},{6,7},{7,6}} | collective-permute-start | bytes 1572872 | tf_op jit(solution)/shard_map/ppermute | solution.py:174

commit v3 on v2

--- a/solution.py
+++ b/solution.py
@@ -13,6 +13,7 @@
 TILE = 256
 PAD = 16
 STEP = 16
+SLOTS = 3
 
 
 def share_kernel(n_grp, n_loc, mine_ref, all_ref, send_sem, recv_sem):
@@ -65,7 +66,7 @@
             acc[s] = v
 
 
-def pass_kernel(n_slots, split, n_local, list_len, n_pad, row_block, x_places, out_places, cnt_ref, list_ref, gate_ref, *refs):
+def pass_kernel(n_slots, n_local, list_len, n_pad, row_block, x_places, out_places, cnt_ref, list_ref, gate_ref, *refs):
     n_x, n_out = len(x_places), len(out_places)
     stride = row_block + 4
     x_hbm, (wg_hbm, wu_hbm, wd_hbm), refs = refs[:n_x], refs[n_x:n_x + 3], refs[n_x + 3:]
@@ -95,9 +96,6 @@
         now = weights(e, slot)
         ahead = weights(e + n_slots, slot)
         n_blocks = jnp.maximum((n + row_block - 1) // row_block, 1)
-        if not split:
-            for copy in now:
-                copy.wait()
 
         def block(b, c):
             base = b * row_block
@@ -112,11 +110,10 @@
             for j in range(d_model // LANES):
                 xg[:, j * LANES:(j + 1) * LANES] = xs[pl.ds(j * stride, row_block), :].astype(jnp.bfloat16)
 
-            if split:
-                @pl.when(b == 0)
-                def _():
-                    now[0].wait()
-                    now[1].wait()
+            @pl.when(b == 0)
+            def _():
+                now[0].wait()
+                now[1].wait()
 
             for q in range(d_ff // TILE):
                 cols = slice(q * TILE, (q + 1) * TILE)
@@ -124,15 +121,14 @@
                 v = jnp.dot(xg[...], wu_ref[slot, :, cols], preferred_element_type=jnp.float32)
                 hid[:, cols] = (jax.nn.silu(u) * v).astype(jnp.bfloat16)
 
-            if split:
-                @pl.when(b == 0)
-                def _():
-                    now[2].wait()
-
-                @pl.when((b == n_blocks - 1) & (e + n_slots < n_local))
-                def _():
-                    ahead[0].start()
-                    ahead[1].start()
+            @pl.when(b == 0)
+            def _():
+                now[2].wait()
+
+            @pl.when((b == n_blocks - 1) & (e + n_slots < n_local))
+            def _():
+                ahead[0].start()
+                ahead[1].start()
 
             for q in range(d_model // TILE):
                 o = jnp.dot(hid[...], wd_ref[slot, :, q * TILE:(q + 1) * TILE], preferred_element_type=jnp.float32)
@@ -150,8 +146,7 @@
 
         @pl.when(e + n_slots < n_local)
         def _():
-            for copy in ahead[2:] if split else ahead:
-                copy.start()
+            ahead[2].start()
 
         return carry
 
@@ -212,8 +207,8 @@
         y_high = swap_loc(high)
         x_low = swap_grp(low, 2)
         x_high = swap_grp(high, 2)
+        late, x_low = lax.optimization_barrier((high, x_low))
         d_low = swap_loc(x_low)
-        late, y_low = lax.optimization_barrier((high, y_low))
         d_high = swap_diag(late)
         parts = {
             0: [low, high],
@@ -227,39 +222,55 @@
         }
 
         cube = meta_all.transpose(1, 0, 2).reshape(2 * top_k, 2, 2, 2, 2, mid)
-        near_keep, near_send = [(0, 0), (0, 1), (1, 0), (1, 1), (2, 0), (3, 0)], [(4, 0), (5, 0)]
-        far_keep, far_send = [(2, 1), (3, 1)], [(4, 1), (5, 1), (6, 0), (6, 1), (7, 0), (7, 1)]
+        near = [(4, 0), (5, 0), (0, 0), (0, 1), (1, 0), (1, 1), (2, 0), (3, 0)]
+        far = [(4, 1), (5, 1), (6, 0), (6, 1), (7, 0), (7, 1), (2, 1), (3, 1)]
 
         def join(*blocks):
             return jnp.concatenate([b.reshape(2 * top_k, -1, mid) for b in blocks], axis=1).reshape(2 * top_k, -1)
 
+        row_block = 144
+        n_rows = len(near) * mid
+        n_pad = n_rows + PAD
+        list_len = -(-min(capacity, n_rows) // row_block) * row_block
+        both = jnp.stack([join(cube[:, 1, 0, :, 0], cube[:, 0, 0], cube[:, 0, 1, :, 0]), join(cube[:, 1, 0, :, 1], cube[:, 1, 1], cube[:, 0, 1, :, 1])])
+        ids = both[:, :top_k].astype(jnp.int32)
+        gates = both[:, top_k:]
+        match = ids[:, None] == (jnp.arange(n_local) + me * n_local)[None, :, None, None]
+        hit = jnp.any(match, axis=2)
+        gate_of = jnp.sum(jnp.where(match, gates[:, None], 0.0), axis=2)
+        gate_of = jnp.pad(gate_of, ((0, 0), (0, 0), (0, PAD)))
+        n_blk = n_rows // LANES
+        lane = jnp.arange(LANES)
+        upper = (lane[:, None] <= lane[None, :]).astype(jnp.bfloat16)
+        inner = jnp.dot(hit.reshape(-1, LANES).astype(jnp.bfloat16), upper, preferred_element_type=jnp.float32)
+        inner = inner.reshape(2, n_local, n_blk, LANES)
+        filled = inner[..., -1].astype(jnp.int32)
+        blk = jnp.arange(n_blk)
+        ends = jnp.sum(jnp.where(blk[:, None] >= blk[None, :], filled[:, :, None, :], 0), axis=3)
+        count = ends[:, :, -1]
+        place = jnp.arange(list_len)
+        past = ends[:, :, None, :] <= place[:, None]
+        which = jnp.sum(past.astype(jnp.int32), axis=3)
+        rest = place - jnp.max(jnp.where(past, ends[:, :, None, :], 0), axis=3)
+        pick = (which[..., None] == blk).astype(jnp.bfloat16)
+        ranks = jnp.einsum("qepb,qebi->qepi", pick, inner.astype(jnp.bfloat16), preferred_element_type=jnp.float32)
+        within = jnp.sum((ranks <= rest[..., None].astype(jnp.float32)).astype(jnp.int32), axis=3)
+        rows = jnp.where(which < n_blk, which * LANES + within, n_rows + place % PAD)
+        feeds = [(count[p], rows[p].reshape(-1), gate_of[p].reshape(-1)) for p in range(2)]
+
         any_spec = pl.BlockSpec(memory_space=pl.ANY)
         piece = jax.ShapeDtypeStruct((mid, chunks, LANES), jnp.float32)
 
-        def run_pass(blocks, meta, row_block, n_slots, split, before=None):
-            n_rows = len(blocks) * mid
-            n_pad = n_rows + PAD
-            list_len = -(-min(capacity, n_rows) // row_block) * row_block
-            ids = meta[:top_k].astype(jnp.int32)
-            gates = meta[top_k:]
-            match = ids[None] == jnp.arange(n_local)[:, None, None] + me * n_local
-            hit = jnp.any(match, axis=1)
-            gate_of = jnp.sum(jnp.where(match, gates[None], 0.0), axis=1)
-            gate_of = jnp.pad(gate_of, ((0, 0), (0, PAD))).reshape(-1)
-            rank = jnp.cumsum(hit.astype(jnp.int32), axis=1)
-            count = rank[:, -1]
-            place = jnp.arange(list_len)[None, :]
-            rows = jnp.sum((rank[:, None, :] <= place[:, :, None]).astype(jnp.int32), axis=2)
-            rows = jnp.where(place < count[:, None], rows, n_rows + place % PAD).reshape(-1)
-
+        def run_pass(p, blocks, before=None):
             x_parts = [parts[r][h] for r, h in blocks]
             x_places = [p * mid for p in range(len(blocks))]
             out_places = x_places
             stride = row_block + 4
+            count_p, rows_p, gates_p = feeds[p]
             if before is not None:
-                count, before = lax.optimization_barrier((count, before))
+                count_p, before = lax.optimization_barrier((count_p, before))
             run = pl.pallas_call(
-                functools.partial(pass_kernel, n_slots, split, n_local, list_len, n_pad, row_block, x_places, out_places),
+                functools.partial(pass_kernel, SLOTS, n_local, list_len, n_pad, row_block, x_places, out_places),
                 grid_spec=pltpu.PrefetchScalarGridSpec(
                     num_scalar_prefetch=3,
                     grid=(),
@@ -271,11 +282,11 @@
                         pltpu.VMEM((chunks * stride, LANES), jnp.float32),
                         pltpu.VMEM((row_block, d_model), jnp.bfloat16),
                         pltpu.VMEM((row_block, d_ff), jnp.bfloat16),
-                        pltpu.VMEM((n_slots, d_model, d_ff), jnp.bfloat16),
-                        pltpu.VMEM((n_slots, d_model, d_ff), jnp.bfloat16),
-                        pltpu.VMEM((n_slots, d_ff, d_model), jnp.bfloat16),
+                        pltpu.VMEM((SLOTS, d_model, d_ff), jnp.bfloat16),
+                        pltpu.VMEM((SLOTS, d_model, d_ff), jnp.bfloat16),
+                        pltpu.VMEM((SLOTS, d_ff, d_model), jnp.bfloat16),
                         pltpu.SemaphoreType.DMA((len(x_parts),)),
-                        pltpu.SemaphoreType.DMA((n_slots, 3)),
+                        pltpu.SemaphoreType.DMA((SLOTS, 3)),
                         pltpu.SemaphoreType.DMA((len(out_places),)),
                     ],
                 ),
@@ -283,11 +294,11 @@
                 compiler_params=pltpu.CompilerParams(vmem_limit_bytes=62_000_000),
                 cost_estimate=pl.CostEstimate(flops=25 * 10**9, bytes_accessed=110 * 10**6, transcendentals=0),
             )
-            outs = run(count, rows, gate_of, *x_parts, w_gate, w_up, w_down)
+            outs = run(count_p, rows_p, gates_p, *x_parts, w_gate, w_up, w_down)
             return {**(before or {}), **dict(zip(blocks, outs))}
 
-        pieces = run_pass(near_send + near_keep, join(cube[:, 1, 0, :, 0], cube[:, 0, 0], cube[:, 0, 1, :, 0]), 144, 3, True)
-        pieces = run_pass(far_send + far_keep, join(cube[:, 1, 0, :, 1], cube[:, 1, 1], cube[:, 0, 1, :, 1]), 144, 3, True, pieces)
+        pieces = run_pass(0, near)
+        pieces = run_pass(1, far, pieces)
 
         totals = [None, None]
         for k, h in [(0, 0), (1, 0), (2, 0), (2, 1), (3, 0), (3, 1), (1, 1), (0, 1)]:

time: 311 us -> 311 us (level)
  other arithmetic: 19.7 us -> 7.53 us
  waiting for transfers between devices: 157 us -> 168 us
    ppermute x1, waiting for transfers between devices: 0.01 us -> 9.17 us  [swap_diag(): return lax.ppermute(a, ('loc', 'grp'), pairs)]
    another operation x6 -> x2, other arithmetic: 6.64 us -> 0.61 us
    convert_element_type x6, other arithmetic: 4.49 us -> 0.82 us  [device_step(): mixed = (keep + swap_loc(send)).astype(jnp.bfloat16)]
    ppermute x16, starting transfers between devices: 26.8 us -> 23.6 us  [swap_grp(): return lax.ppermute(a, 'grp', [(i, i ^ bits) for i in range(n_grp)])]
  transfers between devices with their start and end apart: 28 -> 28, of which waited for: 12 -> 13; matrix products, arithmetic and copies ran while one was open for 7% -> 4% of each run, Pallas kernels for 26% -> 26%
where the time goes in v3:
time: 311 us; the launch traced here: 310 us
  waiting for transfers between devices  168 us (54%)
  Pallas kernels  88.8 us (29%)
  starting transfers between devices  35.6 us (11%)
  other arithmetic  7.53 us (2%)
  local copies, waits for them, and re-layouts  6.59 us (2%)
    ppermute x11, waiting for transfers between devices, swap_loc(): return lax.ppermute(a, 'loc', [(i, i ^ 1) for i in range(n_loc)])  142 us
    pallas_call x2, Pallas kernels, run_pass(): outs = run(count_p, rows_p, gates_p, *x_parts, w_gate, w_up, w_down)  80.3 us
    ppermute x16, starting transfers between devices, swap_grp(): return lax.ppermute(a, 'grp', [(i, i ^ bits) for i in range(n_grp)])  23.6 us
    ppermute x16, waiting for transfers between devices, swap_grp(): return lax.ppermute(a, 'grp', [(i, i ^ bits) for i in range(n_grp)])  16.5 us
    ppermute x11, starting transfers between devices, swap_loc(): return lax.ppermute(a, 'loc', [(i, i ^ 1) for i in range(n_loc)])  9.67 us
    ppermute x1, waiting for transfers between devices, swap_diag(): return lax.ppermute(a, ('loc', 'grp'), pairs)  9.17 us
    pallas_call x1, Pallas kernels, device_step(): pl.pallas_call(functools.partial(share_kernel, n_grp, n_loc), out_shape=j...  8.51 us
  transfers between devices with their start and end apart: 28, of which 13 were waited for; matrix products, arithmetic and copies ran while one was open for 4% of the time, Pallas kernels for 26%

profile of v3, /device:TPU:0, one launch (start us, length us, event | category | flops | bytes accessed | tf_op | source)
XLA Modules:
  0.0 310.0 jit_solution(6261626171585920829)
XLA Ops:
  0.0 0.7 convert_bitcast_fusion
  0.7 1.3 pad_maximum_fusion.3.mine_ref
  2.0 8.5 %share.1 = f32[8,16,256]{2,1,0:T(8,128)} custom-call(f32[16,256]{1,0:T(8,128)} %pad_maximum_fusion.3.mine_ref), custom_call_target="tpu_custom_call" | custom-call | tf_op jit(solution)/shard_map/share/pallas_call | solution.py:190
  10.5 1.3 slice_bitcast_fusion
  11.8 0.1 copy.54
  12.1 1.5 collective-permute-start.4
  13.6 1.5 collective-permute-start
  15.1 0.6 collective-permute-start.15
  15.6 0.5 collective-permute-start.9
  16.2 1.0 reshape.45
  17.5 0.2 compare_reduce_fusion
  17.7 0.2 fusion.1
  17.9 0.1 fusion.5
  18.1 0.4 fusion.3
  18.5 0.3 select_reduce_fusion.1
  18.8 0.3 convert_reduce_fusion.1
  19.2 0.7 reshape_squeeze.23.gate_ref
  19.9 0.7 reshape_squeeze.21.gate_ref
  20.6 3.0 fusion
  23.6 1.4 convert_reduce_fusion
  25.0 1.9 collective-permute-done.4.refs_6_
  26.9 1.5 collective-permute-start.11
  28.5 0.1 collective-permute-start.5
  28.6 8.7 %collective-permute-done.15.refs_6_ = bf16[128,16,128]{2,1,0:T(8,128)(2,1)S(1)} collective-permute-done((bf16[128,16,128]{2,1,0:T(8,128)(2,1)S(1)}, bf16[128,16,128]{2,1,0:T(8,128)(2,1)S(1)}, u32[]{:S(2)}, u32[]{:S(2)}) %collective-permute-start.15) | collective-permute-done | bytes 524320 | tf_op jit(solution)/shard_map/ppermute | solution.py:169
  37.3 2.4 collective-permute-start.12
  39.7 0.8 reshape_squeeze.22.list_ref
  40.5 0.7 reshape_squeeze.20.list_ref
  41.2 0.8 slice_reduce_fusion
  41.9 0.4 collective-permute-start.16
  42.3 9.2 %collective-permute-done.12.refs_3_ = bf16[128,16,128]{2,1,0:T(8,128)(2,1)} collective-permute-done((bf16[128,16,128]{2,1,0:T(8,128)(2,1)S(1)}, bf16[128,16,128]{2,1,0:T(8,128)(2,1)}, u32[]{:S(2)}, u32[]{:S(2)}) %collective-permute-start.12) | collective-permute-done | bytes 524320 | tf_op jit(solution)/shard_map/ppermute | solution.py:176
  51.5 10.3 %collective-permute-done.11.refs_2_ = bf16[128,16,128]{2,1,0:T(8,128)(2,1)} collective-permute-done((bf16[128,16,128]{2,1,0:T(8,128)(2,1)S(1)}, bf16[128,16,128]{2,1,0:T(8,128)(2,1)}, u32[]{:S(2)}, u32[]{:S(2)}) %collective-permute-start.11) | collective-permute-done | bytes 524320 | tf_op jit(solution)/shard_map/ppermute | solution.py:172
  61.8 0.5 collective-permute-start.13
  62.3 40.1 %shard_map.64 = (f32[128,16,128]{2,1,0:T(8,128)}, f32[128,16,128]{2,1,0:T(8,128)}, f32[128,16,128]{2,1,0:T(8,128)}, f32[128,16,128]{2,1,0:T(8,128)}, f32[128,16,...) custom-call(s32[8]{0:T(128)} %get-tuple-element.67.cnt_ref, ...), custom_call_target="tpu_custom_call" | custom-call | flops 24999999488 | bytes 110000000 | tf_op jit(solution)/shard_map/pallas_call | solution.py:297
  102.5 1.5 collective-permute-start.7
  104.0 40.2 %shard_map.65 = (f32[128,16,128]{2,1,0:T(8,128)}, f32[128,16,128]{2,1,0:T(8,128)}, f32[128,16,128]{2,1,0:T(8,128)}, f32[128,16,128]{2,1,0:T(8,128)}, f32[128,16,...) custom-call(s32[8]{0:T(128)} %get-tuple-element.52.cnt_ref, ...), custom_call_target="tpu_custom_call" | custom-call | flops 24999999488 | bytes 110000000 | tf_op jit(solution)/shard_map/pallas_call | solution.py:297
  144.2 0.6 collective-permute-start.17
  144.8 1.4 collective-permute-start.19
  146.3 0.6 collective-permute-start.21
  146.9 1.4 collective-permute-start.23
  148.3 0.6 collective-permute-start.25
  148.9 0.1 add_convert_fusion.8
  149.0 18.8 %collective-permute-done.17 = f32[128,16,128]{2,1,0:T(8,128)S(1)} collective-permute-done((f32[128,16,128]{2,1,0:T(8,128)}, f32[128,16,128]{2,1,0:T(8,128)S(1)}, u32[]{:S(2)}, u32[]{:S(2)}) %collective-permute-start.17) | collective-permute-done | bytes 1048608 | tf_op jit(solution)/shard_map/ppermute | solution.py:172
  167.8 0.1 add_convert_fusion.7
  167.9 22.3 %collective-permute-done.19 = f32[128,16,128]{2,1,0:T(8,128)S(1)} collective-permute-done((f32[128,16,128]{2,1,0:T(8,128)}, f32[128,16,128]{2,1,0:T(8,128)S(1)}, u32[]{:S(2)}, u32[]{:S(2)}) %collective-permute-start.19) | collective-permute-done | bytes 1048608 | tf_op jit(solution)/shard_map/ppermute | solution.py:172
  190.3 0.1 add_convert_fusion.6
  190.4 22.3 %collective-permute-done.21 = f32[128,16,128]{2,1,0:T(8,128)S(1)} collective-permute-done((f32[128,16,128]{2,1,0:T(8,128)}, f32[128,16,128]{2,1,0:T(8,128)S(1)}, u32[]{:S(2)}, u32[]{:S(2)}) %collective-permute-start.21) | collective-permute-done | bytes 1048608 | tf_op jit(solution)/shard_map/ppermute | solution.py:172
  212.7 5.5 %collective-permute-start.8 = (bf16[128,16,128]{2,1,0:T(8,128)(2,1)S(1)}, bf16[128,16,128]{2,1,0:T(8,128)(2,1)S(1)}, u32[]{:S(2)}, u32[]{:S(2)}) collective-permute-start(bf16[128,16,128]{2,1,0:T(8,128)(2,1)S(1)} %add_convert_fusion.8), channel_id=1, source_target_pairs={{0,1},{1,0},{2,3},{3,2},{4,5},{5,4},{6,7},{7,6}} | collective-permute-start | bytes 1572872 | tf_op jit(solution)/shard_map/ppermute | solution.py:169
  218.2 0.1 add_convert_fusion.4
  218.4 16.9 %collective-permute-done.23 = f32[128,16,128]{2,1,0:T(8,128)S(1)} collective-permute-done((f32[128,16,128]{2,1,0:T(8,128)}, f32[128,16,128]{2,1,0:T(8,128)S(1)}, u32[]{:S(2)}, u32[]{:S(2)}) %collective-permute-start.23) | collective-permute-done | bytes 1048608 | tf_op jit(solution)/shard_map/ppermute | solution.py:172
  235.2 4.3 %collective-permute-start.18 = (bf16[128,16,128]{2,1,0:T(8,128)(2,1)S(1)}, bf16[128,16,128]{2,1,0:T(8,128)(2,1)S(1)}, u32[]{:S(2)}, u32[]{:S(2)}) collective-permute-start(bf16[128,16,128]{2,1,0:T(8,128)(2,1)S(1)} %add_convert_fusion.7), channel_id=1, source_target_pairs={{0,2},{1,3},{2,0},{3,1},{4,6},{5,7},{6,4},{7,5}} | collective-permute-start | bytes 1572872 | tf_op jit(solution)/shard_map/ppermute | solution.py:169
  239.6 18.1 %collective-permute-done.25 = f32[128,16,128]{2,1,0:T(8,128)S(1)} collective-permute-done((f32[128,16,128]{2,1,0:T(8,128)}, f32[128,16,128]{2,1,0:T(8,128)S(1)}, u32[]{:S(2)}, u32[]{:S(2)}) %collective-permute-start.25) | collective-permute-done | bytes 1048608 | tf_op jit(solution)/shard_map/ppermute | solution.py:172
  257.7 3.8 %collective-permute-start.20 = (bf16[128,16,128]{2,1,0:T(8,128)(2,1)S(1)}, bf16[128,16,128]{2,1,0:T(8,128)(2,1)S(1)}, u32[]{:S(2)}, u32[]{:S(2)}) collective-permute-start(bf16[128,16,128]{2,1,0:T(8,128)(2,1)S(1)} %add_convert_fusion.6), channel_id=1, source_target_pairs={{0,3},{1,2},{2,1},{3,0},{4,7},{5,6},{6,5},{7,4}} | collective-permute-start | bytes 1572872 | tf_op jit(solution)/shard_map/ppermute | solution.py:169
  261.5 0.1 add_convert_fusion.3
  261.6 0.1 add_convert_fusion.2
  261.8 18.4 %collective-permute-done.6 = f32[128,16,128]{2,1,0:T(8,128)S(1)} collective-permute-done((f32[128,16,128]{2,1,0:T(8,128)}, f32[128,16,128]{2,1,0:T(8,128)S(1)}, u32[]{:S(2)}, u32[]{:S(2)}) %collective-permute-start.6) | collective-permute-done | bytes 1048608 | tf_op jit(solution)/shard_map/ppermute | solution.py:172
  280.2 4.3 %collective-permute-start.22 = (bf16[128,16,128]{2,1,0:T(8,128)(2,1)S(1)}, bf16[128,16,128]{2,1,0:T(8,128)(2,1)S(1)}, u32[]{:S(2)}, u32[]{:S(2)}) collective-permute-start(bf16[128,16,128]{2,1,0:T(8,128)(2,1)S(1)} %add_convert_fusion.4), channel_id=1, source_target_pairs={{0,2},{1,3},{2,0},{3,1},{4,6},{5,7},{6,4},{7,5}} | collective-permute-start | bytes 1572872 | tf_op jit(solution)/shard_map/ppermute | solution.py:169
  284.5 2.5 collective-permute-start.24
  287.0 0.3 add_convert_fusion.5
  287.3 0.1 copy.62
  287.5 15.2 %collective-permute-done.27 = f32[128,16,128]{2,1,0:T(8,128)S(1)} collective-permute-done((f32[128,16,128]{2,1,0:T(8,128)S(1)}, f32[128,16,128]{2,1,0:T(8,128)S(1)}, u32[]{:S(2)}, u32[]{:S(2)}) %collective-permute-start.27) | collective-permute-done | bytes 1048608 | tf_op jit(solution)/shard_map/ppermute | solution.py:172
  302.6 5.9 %collective-permute-done.24 = bf16[128,16,128]{2,1,0:T(8,128)(2,1)S(1)} collective-permute-done((bf16[128,16,128]{2,1,0:T(8,128)(2,1)S(1)}, bf16[128,16,128]{2,1,0:T(8,128)(2,1)S(1)}, u32[]{:S(2)}, u32[]{:S(2)}) %collective-permute-start.24) | collective-permute-done | bytes 524320 | tf_op jit(solution)/shard_map/ppermute | solution.py:169
  308.5 0.3 add_convert_fusion
  308.8 0.1 copy.61
  309.0 1.1 pad_maximum_fusion
  (75 shorter events, 0.5 us)
Async XLA Ops:
  12.0 50.3 %copy-start = (bf16[16,8,16,128]{3,2,1,0:T(8,128)(2,1)}, bf16[16,8,16,128]{3,2,1,0:T(8,128)(2,1)S(1)}, u32[]{:S(2)}) copy-start(bf16[16,8,16,128]{3,2,1,0:T(8,128)(2,1)S(1)} %copy.54) | copy-start | bytes 1572868
  12.1 50.2 %copy-start.1 = (bf16[16,8,16,128]{3,2,1,0:T(8,128)(2,1)}, bf16[16,8,16,128]{3,2,1,0:T(8,128)(2,1)S(1)}, u32[]{:S(2)}) copy-start(bf16[16,8,16,128]{3,2,1,0:T(8,128)(2,1)S(1)} %copy.53) | copy-start | bytes 1572868
  12.1 14.8 %collective-permute-start.4 = (bf16[128,16,128]{2,1,0:T(8,128)(2,1)S(1)}, bf16[128,16,128]{2,1,0:T(8,128)(2,1)S(1)}, u32[]{:S(2)}, u32[]{:S(2)}) collective-permute-start(bf16[128,16,128]{2,1,0:T(8,128)(2,1)S(1)} %bitcast.45), channel_id=1, source_target_pairs={{0,2},{1,3},{2,0},{3,1},{4,6},{5,7},{6,4},{7,5}} | collective-permute-start | bytes 1572872 | tf_op jit(solution)/shard_map/ppermute | solution.py:169
  13.6 13.3 %collective-permute-start.2 = (bf16[128,16,128]{2,1,0:T(8,128)(2,1)S(1)}, bf16[128,16,128]{2,1,0:T(8,128)(2,1)S(1)}, u32[]{:S(2)}, u32[]{:S(2)}) collective-permute-start(bf16[128,16,128]{2,1,0:T(8,128)(2,1)S(1)} %bitcast.46), channel_id=1, source_target_pairs={{0,1},{1,0},{2,3},{3,2},{4,5},{5,4},{6,7},{7,6}} | collective-permute-start | bytes 1572872 | tf_op jit(solution)/shard_map/ppermute | solution.py:169
  13.6 14.9 %collective-permute-start = (bf16[128,16,128]{2,1,0:T(8,128)(2,1)S(1)}, bf16[128,16,128]{2,1,0:T(8,128)(2,1)}, u32[]{:S(2)}, u32[]{:S(2)}) collective-permute-start(bf16[128,16,128]{2,1,0:T(8,128)(2,1)S(1)} %bitcast.47), channel_id=1, source_target_pairs={{0,4},{4,0},{1,5},{5,1},{2,6},{6,2},{3,7},{7,3}} | collective-permute-start | bytes 1572872 | tf_op jit(solution)/shard_map/ppermute | solution.py:172
  15.1 22.2 %collective-permute-start.15 = (bf16[128,16,128]{2,1,0:T(8,128)(2,1)S(1)}, bf16[128,16,128]{2,1,0:T(8,128)(2,1)S(1)}, u32[]{:S(2)}, u32[]{:S(2)}) collective-permute-start(bf16[128,16,128]{2,1,0:T(8,128)(2,1)S(1)} %bitcast.40), channel_id=1, source_target_pairs={{0,2},{1,3},{2,0},{3,1},{4,6},{5,7},{6,4},{7,5}} | collective-permute-start | bytes 1572872 | tf_op jit(solution)/shard_map/ppermute | solution.py:169
  15.6 24.0 %collective-permute-start.9 = (bf16[128,16,128]{2,1,0:T(8,128)(2,1)S(1)}, bf16[128,16,128]{2,1,0:T(8,128)(2,1)S(1)}, u32[]{:S(2)}, u32[]{:S(2)}) collective-permute-start(bf16[128,16,128]{2,1,0:T(8,128)(2,1)S(1)} %bitcast.41), channel_id=1, source_target_pairs={{0,4},{4,0},{1,5},{5,1},{2,6},{6,2},{3,7},{7,3}} | collective-permute-start | bytes 1572872 | tf_op jit(solution)/shard_map/ppermute | solution.py:172
  26.9 35.4 %copy-start.12 = (bf16[128,16,128]{2,1,0:T(8,128)(2,1)}, bf16[128,16,128]{2,1,0:T(8,128)(2,1)S(1)}, u32[]{:S(2)}) copy-start(bf16[128,16,128]{2,1,0:T(8,128)(2,1)S(1)} %collective-permute-done.4.refs_6_) | copy-start | bytes 1572868
  26.9 15.0 %collective-permute-start.3 = (bf16[128,16,128]{2,1,0:T(8,128)(2,1)S(1)}, bf16[128,16,128]{2,1,0:T(8,128)(2,1)}, u32[]{:S(2)}, u32[]{:S(2)}) collective-permute-start(bf16[128,16,128]{2,1,0:T(8,128)(2,1)S(1)} %bitcast.42), channel_id=1, source_target_pairs={{0,1},{1,0},{2,3},{3,2},{4,5},{5,4},{6,7},{7,6}} | collective-permute-start | bytes 1572872 | tf_op jit(solution)/shard_map/ppermute | solution.py:169
  26.9 35.4 %copy-start.13 = (bf16[128,16,128]{2,1,0:T(8,128)(2,1)}, bf16[128,16,128]{2,1,0:T(8,128)(2,1)S(1)}, u32[]{:S(2)}) copy-start(bf16[128,16,128]{2,1,0:T(8,128)(2,1)S(1)} %collective-permute-done.2.refs_4_) | copy-start | bytes 1572868
  26.9 34.8 %collective-permute-start.11 = (bf16[128,16,128]{2,1,0:T(8,128)(2,1)S(1)}, bf16[128,16,128]{2,1,0:T(8,128)(2,1)}, u32[]{:S(2)}, u32[]{:S(2)}) collective-permute-start(bf16[128,16,128]{2,1,0:T(8,128)(2,1)S(1)} %collective-permute-done.4.refs_6_), channel_id=1, source_target_pairs={{0,4},{4,0},{1,5},{5,1},{2,6},{6,2},{3,7},{7,3}} | collective-permute-start | bytes 1572872 | tf_op jit(solution)/shard_map/ppermute | solution.py:172
  28.5 33.3 %collective-permute-start.5 = (bf16[128,16,128]{2,1,0:T(8,128)(2,1)S(1)}, bf16[128,16,128]{2,1,0:T(8,128)(2,1)}, u32[]{:S(2)}, u32[]{:S(2)}) collective-permute-start(bf16[128,16,128]{2,1,0:T(8,128)(2,1)S(1)} %collective-permute-done.4.refs_6_), channel_id=1, source_target_pairs={{0,1},{1,0},{2,3},{3,2},{4,5},{5,4},{6,7},{7,6}} | collective-permute-start | bytes 1572872 | tf_op jit(solution)/shard_map/ppermute | solution.py:169
  37.3 65.1 %copy-start.10 = (bf16[128,16,128]{2,1,0:T(8,128)(2,1)}, bf16[128,16,128]{2,1,0:T(8,128)(2,1)S(1)}, u32[]{:S(2)}) copy-start(bf16[128,16,128]{2,1,0:T(8,128)(2,1)S(1)} %collective-permute-done.15.refs_6_) | copy-start | bytes 1572868
  37.3 14.2 %collective-permute-start.12 = (bf16[128,16,128]{2,1,0:T(8,128)(2,1)S(1)}, bf16[128,16,128]{2,1,0:T(8,128)(2,1)}, u32[]{:S(2)}, u32[]{:S(2)}) collective-permute-start(bf16[128,16,128]{2,1,0:T(8,128)(2,1)S(1)} %bitcast.43), channel_id=1, source_target_pairs={{0,6},{1,7},{2,4},{3,5},{4,2},{5,3},{6,0},{7,1}} | collective-permute-start | bytes 1572872 | tf_op jit(solution)/shard_map/ppermute | solution.py:176
  39.7 62.8 %copy-start.11 = (bf16[128,16,128]{2,1,0:T(8,128)(2,1)}, bf16[128,16,128]{2,1,0:T(8,128)(2,1)S(1)}, u32[]{:S(2)}) copy-start(bf16[128,16,128]{2,1,0:T(8,128)(2,1)S(1)} %collective-permute-done.9.refs_0_) | copy-start | bytes 1572868
  39.7 22.6 %collective-permute-start.1 = (bf16[128,16,128]{2,1,0:T(8,128)(2,1)}, bf16[128,16,128]{2,1,0:T(8,128)(2,1)}, u32[]{:S(2)}, u32[]{:S(2)}) collective-permute-start(bf16[128,16,128]{2,1,0:T(8,128)(2,1)} %collective-permute-done.refs_0_), channel_id=1, source_target_pairs={{0,1},{1,0},{2,3},{3,2},{4,5},{5,4},{6,7},{7,6}} | collective-permute-start | bytes 1572872 | tf_op jit(solution)/shard_map/ppermute | solution.py:169
  41.9 62.1 %collective-permute-start.16 = (bf16[128,16,128]{2,1,0:T(8,128)(2,1)S(1)}, bf16[128,16,128]{2,1,0:T(8,128)(2,1)}, u32[]{:S(2)}, u32[]{:S(2)}) collective-permute-start(bf16[128,16,128]{2,1,0:T(8,128)(2,1)S(1)} %collective-permute-done.15.refs_6_), channel_id=1, source_target_pairs={{0,1},{1,0},{2,3},{3,2},{4,5},{5,4},{6,7},{7,6}} | collective-permute-start | bytes 1572872 | tf_op jit(solution)/shard_map/ppermute | solution.py:169
  51.5 52.5 %collective-permute-start.10 = (bf16[128,16,128]{2,1,0:T(8,128)(2,1)S(1)}, bf16[128,16,128]{2,1,0:T(8,128)(2,1)}, u32[]{:S(2)}, u32[]{:S(2)}) collective-permute-start(bf16[128,16,128]{2,1,0:T(8,128)(2,1)S(1)} %collective-permute-done.9.refs_0_), channel_id=1, source_target_pairs={{0,1},{1,0},{2,3},{3,2},{4,5},{5,4},{6,7},{7,6}} | collective-permute-start | bytes 1572872 | tf_op jit(solution)/shard_map/ppermute | solution.py:169
  61.8 42.2 %collective-permute-start.14 = (bf16[128,16,128]{2,1,0:T(8,128)(2,1)}, bf16[128,16,128]{2,1,0:T(8,128)(2,1)}, u32[]{:S(2)}, u32[]{:S(2)}) collective-permute-start(bf16[128,16,128]{2,1,0:T(8,128)(2,1)} %collective-permute-done.12.refs_3_), channel_id=1, source_target_pairs={{0,1},{1,0},{2,3},{3,2},{4,5},{5,4},{6,7},{7,6}} | collective-permute-start | bytes 1572872 | tf_op jit(solution)/shard_map/ppermute | solution.py:169
  61.8 42.2 %collective-permute-start.13 = (bf16[128,16,128]{2,1,0:T(8,128)(2,1)}, bf16[128,16,128]{2,1,0:T(8,128)(2,1)}, u32[]{:S(2)}, u32[]{:S(2)}) collective-permute-start(bf16[128,16,128]{2,1,0:T(8,128)(2,1)} %collective-permute-done.11.refs_2_), channel_id=1, source_target_pairs={{0,1},{1,0},{2,3},{3,2},{4,5},{5,4},{6,7},{7,6}} | collective-permute-start | bytes 1572872 | tf_op jit(solution)/shard_map/ppermute | solution.py:169
  102.4 46.4 %copy-start.6 = (f32[128,16,128]{2,1,0:T(8,128)S(1)}, f32[128,16,128]{2,1,0:T(8,128)}, u32[]{:S(2)}) copy-start(f32[128,16,128]{2,1,0:T(8,128)} %get-tuple-element.49) | copy-start | bytes 3145732
  102.5 65.3 %copy-start.4 = (f32[128,16,128]{2,1,0:T(8,128)S(1)}, f32[128,16,128]{2,1,0:T(8,128)}, u32[]{:S(2)}) copy-start(f32[128,16,128]{2,1,0:T(8,128)} %get-tuple-element.51) | copy-start | bytes 3145732
  102.5 45.8 %collective-permute-start.7 = (f32[128,16,128]{2,1,0:T(8,128)}, f32[128,16,128]{2,1,0:T(8,128)S(1)}, u32[]{:S(2)}, u32[]{:S(2)}) collective-permute-start(f32[128,16,128]{2,1,0:T(8,128)} %get-tuple-element.50), channel_id=1, source_target_pairs={{0,4},{4,0},{1,5},{5,1},{2,6},{6,2},{3,7},{7,3}} | collective-permute-start | bytes 3145736 | tf_op jit(solution)/shard_map/ppermute | solution.py:172
  144.2 46.1 %copy-start.14 = (f32[128,16,128]{2,1,0:T(8,128)S(1)}, f32[128,16,128]{2,1,0:T(8,128)}, u32[]{:S(2)}) copy-start(f32[128,16,128]{2,1,0:T(8,128)} %get-tuple-element.64) | copy-start | bytes 3145732
  144.2 46.1 %copy-start.3 = (f32[128,16,128]{2,1,0:T(8,128)S(1)}, f32[128,16,128]{2,1,0:T(8,128)}, u32[]{:S(2)}) copy-start(f32[128,16,128]{2,1,0:T(8,128)} %get-tuple-element.55) | copy-start | bytes 3145732
  144.2 74.0 %copy-start.7 = (f32[128,16,128]{2,1,0:T(8,128)S(1)}, f32[128,16,128]{2,1,0:T(8,128)}, u32[]{:S(2)}) copy-start(f32[128,16,128]{2,1,0:T(8,128)} %get-tuple-element.57) | copy-start | bytes 3145732
  144.2 23.6 %collective-permute-start.17 = (f32[128,16,128]{2,1,0:T(8,128)}, f32[128,16,128]{2,1,0:T(8,128)S(1)}, u32[]{:S(2)}, u32[]{:S(2)}) collective-permute-start(f32[128,16,128]{2,1,0:T(8,128)} %get-tuple-element.54), channel_id=1, source_target_pairs={{0,4},{4,0},{1,5},{5,1},{2,6},{6,2},{3,7},{7,3}} | collective-permute-start | bytes 3145736 | tf_op jit(solution)/shard_map/ppermute | solution.py:172
  144.8 45.4 %collective-permute-start.19 = (f32[128,16,128]{2,1,0:T(8,128)}, f32[128,16,128]{2,1,0:T(8,128)S(1)}, u32[]{:S(2)}, u32[]{:S(2)}) collective-permute-start(f32[128,16,128]{2,1,0:T(8,128)} %get-tuple-element.56), channel_id=1, source_target_pairs={{0,4},{4,0},{1,5},{5,1},{2,6},{6,2},{3,7},{7,3}} | collective-permute-start | bytes 3145736 | tf_op jit(solution)/shard_map/ppermute | solution.py:172
  146.3 66.5 %collective-permute-start.21 = (f32[128,16,128]{2,1,0:T(8,128)}, f32[128,16,128]{2,1,0:T(8,128)S(1)}, u32[]{:S(2)}, u32[]{:S(2)}) collective-permute-start(f32[128,16,128]{2,1,0:T(8,128)} %get-tuple-element.58), channel_id=1, source_target_pairs={{0,4},{4,0},{1,5},{5,1},{2,6},{6,2},{3,7},{7,3}} | collective-permute-start | bytes 3145736 | tf_op jit(solution)/shard_map/ppermute | solution.py:172
  146.9 88.4 %collective-permute-start.23 = (f32[128,16,128]{2,1,0:T(8,128)}, f32[128,16,128]{2,1,0:T(8,128)S(1)}, u32[]{:S(2)}, u32[]{:S(2)}) collective-permute-start(f32[128,16,128]{2,1,0:T(8,128)} %get-tuple-element.60), channel_id=1, source_target_pairs={{0,4},{4,0},{1,5},{5,1},{2,6},{6,2},{3,7},{7,3}} | collective-permute-start | bytes 3145736 | tf_op jit(solution)/shard_map/ppermute | solution.py:172
  148.3 113.2 %copy-start.5 = (f32[128,16,128]{2,1,0:T(8,128)S(1)}, f32[128,16,128]{2,1,0:T(8,128)}, u32[]{:S(2)}) copy-start(f32[128,16,128]{2,1,0:T(8,128)} %get-tuple-element.59) | copy-start | bytes 3145732
  148.3 109.4 %collective-permute-start.25 = (f32[128,16,128]{2,1,0:T(8,128)}, f32[128,16,128]{2,1,0:T(8,128)S(1)}, u32[]{:S(2)}, u32[]{:S(2)}) collective-permute-start(f32[128,16,128]{2,1,0:T(8,128)} %get-tuple-element.62), channel_id=1, source_target_pairs={{0,4},{4,0},{1,5},{5,1},{2,6},{6,2},{3,7},{7,3}} | collective-permute-start | bytes 3145736 | tf_op jit(solution)/shard_map/ppermute | solution.py:172
  149.0 112.6 %copy-start.2 = (f32[128,16,128]{2,1,0:T(8,128)S(1)}, f32[128,16,128]{2,1,0:T(8,128)}, u32[]{:S(2)}) copy-start(f32[128,16,128]{2,1,0:T(8,128)} %get-tuple-element.61) | copy-start | bytes 3145732
  167.8 112.4 %collective-permute-start.6 = (f32[128,16,128]{2,1,0:T(8,128)}, f32[128,16,128]{2,1,0:T(8,128)S(1)}, u32[]{:S(2)}, u32[]{:S(2)}) collective-permute-start(f32[128,16,128]{2,1,0:T(8,128)} %get-tuple-element.48), channel_id=1, source_target_pairs={{0,4},{4,0},{1,5},{5,1},{2,6},{6,2},{3,7},{7,3}} | collective-permute-start | bytes 3145736 | tf_op jit(solution)/shard_map/ppermute | solution.py:172
  190.3 96.7 %copy-start.9 = (f32[128,16,128]{2,1,0:T(8,128)S(1)}, f32[128,16,128]{2,1,0:T(8,128)}, u32[]{:S(2)}) copy-start(f32[128,16,128]{2,1,0:T(8,128)} %get-tuple-element.47) | copy-start | bytes 3145732
  190.3 112.3 %collective-permute-start.27 = (f32[128,16,128]{2,1,0:T(8,128)S(1)}, f32[128,16,128]{2,1,0:T(8,128)S(1)}, u32[]{:S(2)}, u32[]{:S(2)}) collective-permute-start(f32[128,16,128]{2,1,0:T(8,128)S(1)} %copy-done.14), channel_id=1, source_target_pairs={{0,4},{4,0},{1,5},{5,1},{2,6},{6,2},{3,7},{7,3}} | collective-permute-start | bytes 3145736 | tf_op jit(solution)/shard_map/ppermute | solution.py:172
  212.7 71.8 %collective-permute-start.8 = (bf16[128,16,128]{2,1,0:T(8,128)(2,1)S(1)}, bf16[128,16,128]{2,1,0:T(8,128)(2,1)S(1)}, u32[]{:S(2)}, u32[]{:S(2)}) collective-permute-start(bf16[128,16,128]{2,1,0:T(8,128)(2,1)S(1)} %add_convert_fusion.8), channel_id=1, source_target_pairs={{0,1},{1,0},{2,3},{3,2},{4,5},{5,4},{6,7},{7,6}} | collective-permute-start | bytes 1572872 | tf_op jit(solution)/shard_map/ppermute | solution.py:169
  235.2 51.8 %collective-permute-start.18 = (bf16[128,16,128]{2,1,0:T(8,128)(2,1)S(1)}, bf16[128,16,128]{2,1,0:T(8,128)(2,1)S(1)}, u32[]{:S(2)}, u32[]{:S(2)}) collective-permute-start(bf16[128,16,128]{2,1,0:T(8,128)(2,1)S(1)} %add_convert_fusion.7), channel_id=1, source_target_pairs={{0,2},{1,3},{2,0},{3,1},{4,6},{5,7},{6,4},{7,5}} | collective-permute-start | bytes 1572872 | tf_op jit(solution)/shard_map/ppermute | solution.py:169
  257.7 29.3 %collective-permute-start.20 = (bf16[128,16,128]{2,1,0:T(8,128)(2,1)S(1)}, bf16[128,16,128]{2,1,0:T(8,128)(2,1)S(1)}, u32[]{:S(2)}, u32[]{:S(2)}) collective-permute-start(bf16[128,16,128]{2,1,0:T(8,128)(2,1)S(1)} %add_convert_fusion.6), channel_id=1, source_target_pairs={{0,3},{1,2},{2,1},{3,0},{4,7},{5,6},{6,5},{7,4}} | collective-permute-start | bytes 1572872 | tf_op jit(solution)/shard_map/ppermute | solution.py:169
  261.5 47.1 %copy-start.8 = (f32[128,16,128]{2,1,0:T(8,128)S(1)}, f32[128,16,128]{2,1,0:T(8,128)}, u32[]{:S(2)}) copy-start(f32[128,16,128]{2,1,0:T(8,128)} %get-tuple-element.63) | copy-start | bytes 3145732
  280.2 22.5 %collective-permute-start.22 = (bf16[128,16,128]{2,1,0:T(8,128)(2,1)S(1)}, bf16[128,16,128]{2,1,0:T(8,128)(2,1)S(1)}, u32[]{:S(2)}, u32[]{:S(2)}) collective-permute-start(bf16[128,16,128]{2,1,0:T(8,128)(2,1)S(1)} %add_convert_fusion.4), channel_id=1, source_target_pairs={{0,2},{1,3},{2,0},{3,1},{4,6},{5,7},{6,4},{7,5}} | collective-permute-start | bytes 1572872 | tf_op jit(solution)/shard_map/ppermute | solution.py:169
  284.5 24.0 %collective-permute-start.24 = (bf16[128,16,128]{2,1,0:T(8,128)(2,1)S(1)}, bf16[128,16,128]{2,1,0:T(8,128)(2,1)S(1)}, u32[]{:S(2)}, u32[]{:S(2)}) collective-permute-start(bf16[128,16,128]{2,1,0:T(8,128)(2,1)S(1)} %add_convert_fusion.3), channel_id=1, source_target_pairs={{0,3},{1,2},{2,1},{3,0},{4,7},{5,6},{6,5},{7,4}} | collective-permute-start | bytes 1572872 | tf_op jit(solution)/shard_map/ppermute | solution.py:169
  287.0 21.5 %collective-permute-start.26 = (bf16[128,16,128]{2,1,0:T(8,128)(2,1)S(1)}, bf16[128,16,128]{2,1,0:T(8,128)(2,1)S(1)}, u32[]{:S(2)}, u32[]{:S(2)}) collective-permute-start(bf16[128,16,128]{2,1,0:T(8,128)(2,1)S(1)} %add_convert_fusion.2), channel_id=1, source_target_pairs={{0,1},{1,0},{2,3},{3,2},{4,5},{5,4},{6,7},{7,6}} | collective-permute-start | bytes 1572872 | tf_op jit(solution)/shard_map/ppermute | solution.py:169

commit v4 on v3

--- a/solution.py
+++ b/solution.py
@@ -16,13 +16,16 @@
 SLOTS = 3
 
 
-def share_kernel(n_grp, n_loc, mine_ref, all_ref, send_sem, recv_sem):
+def share_kernel(n_grp, n_loc, ids_ref, gate_ref, all_ref, mine_ref, send_sem, recv_sem):
     grp, loc = lax.axis_index("grp"), lax.axis_index("loc")
     n_dev = n_grp * n_loc
 
     def peer(r):
         return {"grp": grp ^ (r % n_grp), "loc": loc ^ (r // n_grp)}
 
+    top_k = ids_ref.shape[0]
+    mine_ref[:top_k, :] = ids_ref[...].astype(jnp.float32)
+    mine_ref[top_k:, :] = gate_ref[...]
     barrier = pltpu.get_barrier_semaphore()
     for r in range(1, n_dev):
         pl.semaphore_signal(barrier, inc=1, device_id=peer(r), device_id_type=MESH)
@@ -186,16 +189,15 @@
         capacity = 8 * (n_tok * top_k // (4 * per_group * n_grp) + 1)
         me = lax.axis_index("grp") * n_loc + lax.axis_index("loc")
 
-        meta = jnp.concatenate([expert_ids.astype(jnp.float32).T, gate_val.T], axis=0)
         meta_all = pl.pallas_call(
             functools.partial(share_kernel, n_grp, n_loc),
-            out_shape=jax.ShapeDtypeStruct((n_dev,) + meta.shape, jnp.float32),
-            in_specs=[pl.BlockSpec(memory_space=pltpu.VMEM)],
+            out_shape=jax.ShapeDtypeStruct((n_dev, 2 * top_k, tok_local), jnp.float32),
+            in_specs=[pl.BlockSpec(memory_space=pltpu.VMEM)] * 2,
             out_specs=pl.BlockSpec(memory_space=pltpu.VMEM),
-            scratch_shapes=[pltpu.SemaphoreType.DMA((n_dev,)), pltpu.SemaphoreType.DMA((n_dev,))],
+            scratch_shapes=[pltpu.VMEM((2 * top_k, tok_local), jnp.float32), pltpu.SemaphoreType.DMA((n_dev,)), pltpu.SemaphoreType.DMA((n_dev,))],
             compiler_params=pltpu.CompilerParams(collective_id=0, has_side_effects=True),
             name="share",
-        )(meta)
+        )(expert_ids.T, gate_val.T)
         mid = tok_local // 2
         low, high = (x_tok[h * mid:(h + 1) * mid].reshape(mid, chunks, LANES) for h in range(2))
         low, high, meta_all = lax.optimization_barrier((low, high, meta_all))

time: 311 us -> 309 us (level)
  no operation moved by 1% of the time
where the time goes in v4:
time: 309 us; the launch traced here: 308 us
  waiting for transfers between devices  168 us (54%)
  Pallas kernels  88.9 us (29%)
  starting transfers between devices  35.2 us (11%)
  local copies, waits for them, and re-layouts  6.55 us (2%)
  other arithmetic  5.53 us (2%)
  matrix products  3.1 us (1%)
    ppermute x11, waiting for transfers between devices, swap_loc(): return lax.ppermute(a, 'loc', [(i, i ^ 1) for i in range(n_loc)])  143 us
    pallas_call x2, Pallas kernels, run_pass(): outs = run(count_p, rows_p, gates_p, *x_parts, w_gate, w_up, w_down)  80.3 us
    ppermute x16, starting transfers between devices, swap_grp(): return lax.ppermute(a, 'grp', [(i, i ^ bits) for i in range(n_grp)])  23.2 us
    ppermute x16, waiting for transfers between devices, swap_grp(): return lax.ppermute(a, 'grp', [(i, i ^ bits) for i in range(n_grp)])  16.4 us
    ppermute x11, starting transfers between devices, swap_loc(): return lax.ppermute(a, 'loc', [(i, i ^ 1) for i in range(n_loc)])  9.65 us
    ppermute x1, waiting for transfers between devices, swap_diag(): return lax.ppermute(a, ('loc', 'grp'), pairs)  9.17 us
    pallas_call x1, Pallas kernels, device_step(): pl.pallas_call(functools.partial(share_kernel, n_grp, n_loc), out_shape=j...  8.59 us
  transfers between devices with their start and end apart: 28, of which 13 were waited for; matrix products, arithmetic and copies ran while one was open for 4% of the time, Pallas kernels for 26%

profile of v4, /device:TPU:0, one launch (start us, length us, event | category | flops | bytes accessed | tf_op | source)
XLA Modules:
  0.0 308.1 jit_solution(454015736377839648)
XLA Ops:
  0.0 1.3 slice_bitcast_fusion
  1.3 0.1 copy.54
  1.4 0.1 copy.53
  1.5 8.6 %share.1 = f32[8,16,256]{2,1,0:T(8,128)} custom-call(s32[8,256]{1,0:T(8,128)} %bitcast.60, f32[8,256]{1,0:T(8,128)} %bitcast.61), custom_call_target="tpu_custom_call" | custom-call | tf_op jit(solution)/shard_map/share/pallas_call | solution.py:192
  10.1 1.5 collective-permute-start.4
  11.6 1.5 collective-permute-start
  13.1 0.6 collective-permute-start.15
  13.7 0.5 collective-permute-start.9
  14.2 1.0 reshape.45
  15.5 0.2 compare_reduce_fusion
  15.7 0.2 fusion.1
  16.0 0.1 fusion.5
  16.1 0.4 fusion.3
  16.5 0.3 select_reduce_fusion.1
  16.9 0.3 convert_reduce_fusion.1
  17.2 0.7 reshape_squeeze.23.gate_ref
  17.9 0.7 reshape_squeeze.21.gate_ref
  18.6 3.0 fusion
  21.6 1.4 convert_reduce_fusion
  23.0 1.9 collective-permute-done.4.refs_6_
  25.0 1.5 collective-permute-start.11
  26.5 0.1 collective-permute-done.refs_0_
  26.5 0.1 collective-permute-start.5
  26.7 8.7 %collective-permute-done.15.refs_6_ = bf16[128,16,128]{2,1,0:T(8,128)(2,1)S(1)} collective-permute-done((bf16[128,16,128]{2,1,0:T(8,128)(2,1)S(1)}, bf16[128,16,128]{2,1,0:T(8,128)(2,1)S(1)}, u32[]{:S(2)}, u32[]{:S(2)}) %collective-permute-start.15) | collective-permute-done | bytes 524320 | tf_op jit(solution)/shard_map/ppermute | solution.py:172
  35.3 2.4 collective-permute-start.12
  37.8 0.8 reshape_squeeze.22.list_ref
  38.5 0.7 reshape_squeeze.20.list_ref
  39.2 0.8 slice_reduce_fusion
  40.0 0.4 collective-permute-start.16
  40.4 9.2 %collective-permute-done.12.refs_3_ = bf16[128,16,128]{2,1,0:T(8,128)(2,1)} collective-permute-done((bf16[128,16,128]{2,1,0:T(8,128)(2,1)S(1)}, bf16[128,16,128]{2,1,0:T(8,128)(2,1)}, u32[]{:S(2)}, u32[]{:S(2)}) %collective-permute-start.12) | collective-permute-done | bytes 524320 | tf_op jit(solution)/shard_map/ppermute | solution.py:179
  49.5 10.3 %collective-permute-done.11.refs_2_ = bf16[128,16,128]{2,1,0:T(8,128)(2,1)} collective-permute-done((bf16[128,16,128]{2,1,0:T(8,128)(2,1)S(1)}, bf16[128,16,128]{2,1,0:T(8,128)(2,1)}, u32[]{:S(2)}, u32[]{:S(2)}) %collective-permute-start.11) | collective-permute-done | bytes 524320 | tf_op jit(solution)/shard_map/ppermute | solution.py:175
  59.8 0.5 collective-permute-start.13
  60.3 40.1 %shard_map.64 = (f32[128,16,128]{2,1,0:T(8,128)}, f32[128,16,128]{2,1,0:T(8,128)}, f32[128,16,128]{2,1,0:T(8,128)}, f32[128,16,128]{2,1,0:T(8,128)}, f32[128,16,...) custom-call(s32[8]{0:T(128)} %get-tuple-element.67.cnt_ref, ...), custom_call_target="tpu_custom_call" | custom-call | flops 24999999488 | bytes 110000000 | tf_op jit(solution)/shard_map/pallas_call | solution.py:299
  100.5 1.6 collective-permute-start.7
  102.1 40.2 %shard_map.65 = (f32[128,16,128]{2,1,0:T(8,128)}, f32[128,16,128]{2,1,0:T(8,128)}, f32[128,16,128]{2,1,0:T(8,128)}, f32[128,16,128]{2,1,0:T(8,128)}, f32[128,16,...) custom-call(s32[8]{0:T(128)} %get-tuple-element.52.cnt_ref, ...), custom_call_target="tpu_custom_call" | custom-call | flops 24999999488 | bytes 110000000 | tf_op jit(solution)/shard_map/pallas_call | solution.py:299
  142.3 0.5 collective-permute-start.17
  142.8 1.5 collective-permute-start.19
  144.4 0.5 collective-permute-start.21
  144.8 1.5 collective-permute-start.23
  146.4 0.5 collective-permute-start.25
  146.9 0.1 add_convert_fusion.8
  147.0 18.9 %collective-permute-done.17 = f32[128,16,128]{2,1,0:T(8,128)S(1)} collective-permute-done((f32[128,16,128]{2,1,0:T(8,128)}, f32[128,16,128]{2,1,0:T(8,128)S(1)}, u32[]{:S(2)}, u32[]{:S(2)}) %collective-permute-start.17) | collective-permute-done | bytes 1048608 | tf_op jit(solution)/shard_map/ppermute | solution.py:175
  166.0 0.1 add_convert_fusion.7
  166.1 22.3 %collective-permute-done.19 = f32[128,16,128]{2,1,0:T(8,128)S(1)} collective-permute-done((f32[128,16,128]{2,1,0:T(8,128)}, f32[128,16,128]{2,1,0:T(8,128)S(1)}, u32[]{:S(2)}, u32[]{:S(2)}) %collective-permute-start.19) | collective-permute-done | bytes 1048608 | tf_op jit(solution)/shard_map/ppermute | solution.py:175
  188.4 0.1 add_convert_fusion.6
  188.6 22.3 %collective-permute-done.21 = f32[128,16,128]{2,1,0:T(8,128)S(1)} collective-permute-done((f32[128,16,128]{2,1,0:T(8,128)}, f32[128,16,128]{2,1,0:T(8,128)S(1)}, u32[]{:S(2)}, u32[]{:S(2)}) %collective-permute-start.21) | collective-permute-done | bytes 1048608 | tf_op jit(solution)/shard_map/ppermute | solution.py:175
  210.9 5.4 %collective-permute-start.8 = (bf16[128,16,128]{2,1,0:T(8,128)(2,1)S(1)}, bf16[128,16,128]{2,1,0:T(8,128)(2,1)S(1)}, u32[]{:S(2)}, u32[]{:S(2)}) collective-permute-start(bf16[128,16,128]{2,1,0:T(8,128)(2,1)S(1)} %add_convert_fusion.8), channel_id=1, source_target_pairs={{0,1},{1,0},{2,3},{3,2},{4,5},{5,4},{6,7},{7,6}} | collective-permute-start | bytes 1572872 | tf_op jit(solution)/shard_map/ppermute | solution.py:172
  216.3 0.1 add_convert_fusion.4
  216.4 17.0 %collective-permute-done.23 = f32[128,16,128]{2,1,0:T(8,128)S(1)} collective-permute-done((f32[128,16,128]{2,1,0:T(8,128)}, f32[128,16,128]{2,1,0:T(8,128)S(1)}, u32[]{:S(2)}, u32[]{:S(2)}) %collective-permute-start.23) | collective-permute-done | bytes 1048608 | tf_op jit(solution)/shard_map/ppermute | solution.py:175
  233.4 4.3 %collective-permute-start.18 = (bf16[128,16,128]{2,1,0:T(8,128)(2,1)S(1)}, bf16[128,16,128]{2,1,0:T(8,128)(2,1)S(1)}, u32[]{:S(2)}, u32[]{:S(2)}) collective-permute-start(bf16[128,16,128]{2,1,0:T(8,128)(2,1)S(1)} %add_convert_fusion.7), channel_id=1, source_target_pairs={{0,2},{1,3},{2,0},{3,1},{4,6},{5,7},{6,4},{7,5}} | collective-permute-start | bytes 1572872 | tf_op jit(solution)/shard_map/ppermute | solution.py:172
  237.6 18.2 %collective-permute-done.25 = f32[128,16,128]{2,1,0:T(8,128)S(1)} collective-permute-done((f32[128,16,128]{2,1,0:T(8,128)}, f32[128,16,128]{2,1,0:T(8,128)S(1)}, u32[]{:S(2)}, u32[]{:S(2)}) %collective-permute-start.25) | collective-permute-done | bytes 1048608 | tf_op jit(solution)/shard_map/ppermute | solution.py:175
  255.8 3.7 %collective-permute-start.20 = (bf16[128,16,128]{2,1,0:T(8,128)(2,1)S(1)}, bf16[128,16,128]{2,1,0:T(8,128)(2,1)S(1)}, u32[]{:S(2)}, u32[]{:S(2)}) collective-permute-start(bf16[128,16,128]{2,1,0:T(8,128)(2,1)S(1)} %add_convert_fusion.6), channel_id=1, source_target_pairs={{0,3},{1,2},{2,1},{3,0},{4,7},{5,6},{6,5},{7,4}} | collective-permute-start | bytes 1572872 | tf_op jit(solution)/shard_map/ppermute | solution.py:172
  259.5 0.1 add_convert_fusion.3
  259.7 0.1 add_convert_fusion.2
  259.8 18.5 %collective-permute-done.6 = f32[128,16,128]{2,1,0:T(8,128)S(1)} collective-permute-done((f32[128,16,128]{2,1,0:T(8,128)}, f32[128,16,128]{2,1,0:T(8,128)S(1)}, u32[]{:S(2)}, u32[]{:S(2)}) %collective-permute-start.6) | collective-permute-done | bytes 1048608 | tf_op jit(solution)/shard_map/ppermute | solution.py:175
  278.3 4.3 %collective-permute-start.22 = (bf16[128,16,128]{2,1,0:T(8,128)(2,1)S(1)}, bf16[128,16,128]{2,1,0:T(8,128)(2,1)S(1)}, u32[]{:S(2)}, u32[]{:S(2)}) collective-permute-start(bf16[128,16,128]{2,1,0:T(8,128)(2,1)S(1)} %add_convert_fusion.4), channel_id=1, source_target_pairs={{0,2},{1,3},{2,0},{3,1},{4,6},{5,7},{6,4},{7,5}} | collective-permute-start | bytes 1572872 | tf_op jit(solution)/shard_map/ppermute | solution.py:172
  282.6 2.5 collective-permute-start.24
  285.0 0.3 add_convert_fusion.5
  285.4 0.1 copy.62
  285.5 15.3 %collective-permute-done.27 = f32[128,16,128]{2,1,0:T(8,128)S(1)} collective-permute-done((f32[128,16,128]{2,1,0:T(8,128)S(1)}, f32[128,16,128]{2,1,0:T(8,128)S(1)}, u32[]{:S(2)}, u32[]{:S(2)}) %collective-permute-start.27) | collective-permute-done | bytes 1048608 | tf_op jit(solution)/shard_map/ppermute | solution.py:175
  300.8 5.8 %collective-permute-done.24 = bf16[128,16,128]{2,1,0:T(8,128)(2,1)S(1)} collective-permute-done((bf16[128,16,128]{2,1,0:T(8,128)(2,1)S(1)}, bf16[128,16,128]{2,1,0:T(8,128)(2,1)S(1)}, u32[]{:S(2)}, u32[]{:S(2)}) %collective-permute-start.24) | collective-permute-done | bytes 524320 | tf_op jit(solution)/shard_map/ppermute | solution.py:172
  306.6 0.3 add_convert_fusion
  306.9 0.1 copy.61
  307.0 1.1 pad_maximum_fusion
  (73 shorter events, 0.4 us)
Async XLA Ops:
  1.4 58.9 %copy-start = (bf16[16,8,16,128]{3,2,1,0:T(8,128)(2,1)}, bf16[16,8,16,128]{3,2,1,0:T(8,128)(2,1)S(1)}, u32[]{:S(2)}) copy-start(bf16[16,8,16,128]{3,2,1,0:T(8,128)(2,1)S(1)} %copy.54) | copy-start | bytes 1572868
  1.5 58.8 %copy-start.1 = (bf16[16,8,16,128]{3,2,1,0:T(8,128)(2,1)}, bf16[16,8,16,128]{3,2,1,0:T(8,128)(2,1)S(1)}, u32[]{:S(2)}) copy-start(bf16[16,8,16,128]{3,2,1,0:T(8,128)(2,1)S(1)} %copy.53) | copy-start | bytes 1572868
  10.1 14.8 %collective-permute-start.4 = (bf16[128,16,128]{2,1,0:T(8,128)(2,1)S(1)}, bf16[128,16,128]{2,1,0:T(8,128)(2,1)S(1)}, u32[]{:S(2)}, u32[]{:S(2)}) collective-permute-start(bf16[128,16,128]{2,1,0:T(8,128)(2,1)S(1)} %bitcast.44), channel_id=1, source_target_pairs={{0,2},{1,3},{2,0},{3,1},{4,6},{5,7},{6,4},{7,5}} | collective-permute-start | bytes 1572872 | tf_op jit(solution)/shard_map/ppermute | solution.py:172
  11.6 13.3 %collective-permute-start.2 = (bf16[128,16,128]{2,1,0:T(8,128)(2,1)S(1)}, bf16[128,16,128]{2,1,0:T(8,128)(2,1)S(1)}, u32[]{:S(2)}, u32[]{:S(2)}) collective-permute-start(bf16[128,16,128]{2,1,0:T(8,128)(2,1)S(1)} %bitcast.45), channel_id=1, source_target_pairs={{0,1},{1,0},{2,3},{3,2},{4,5},{5,4},{6,7},{7,6}} | collective-permute-start | bytes 1572872 | tf_op jit(solution)/shard_map/ppermute | solution.py:172
  11.6 14.9 %collective-permute-start = (bf16[128,16,128]{2,1,0:T(8,128)(2,1)S(1)}, bf16[128,16,128]{2,1,0:T(8,128)(2,1)}, u32[]{:S(2)}, u32[]{:S(2)}) collective-permute-start(bf16[128,16,128]{2,1,0:T(8,128)(2,1)S(1)} %bitcast.46), channel_id=1, source_target_pairs={{0,4},{4,0},{1,5},{5,1},{2,6},{6,2},{3,7},{7,3}} | collective-permute-start | bytes 1572872 | tf_op jit(solution)/shard_map/ppermute | solution.py:175
  13.1 22.2 %collective-permute-start.15 = (bf16[128,16,128]{2,1,0:T(8,128)(2,1)S(1)}, bf16[128,16,128]{2,1,0:T(8,128)(2,1)S(1)}, u32[]{:S(2)}, u32[]{:S(2)}) collective-permute-start(bf16[128,16,128]{2,1,0:T(8,128)(2,1)S(1)} %bitcast.39), channel_id=1, source_target_pairs={{0,2},{1,3},{2,0},{3,1},{4,6},{5,7},{6,4},{7,5}} | collective-permute-start | bytes 1572872 | tf_op jit(solution)/shard_map/ppermute | solution.py:172
  13.7 24.0 %collective-permute-start.9 = (bf16[128,16,128]{2,1,0:T(8,128)(2,1)S(1)}, bf16[128,16,128]{2,1,0:T(8,128)(2,1)S(1)}, u32[]{:S(2)}, u32[]{:S(2)}) collective-permute-start(bf16[128,16,128]{2,1,0:T(8,128)(2,1)S(1)} %bitcast.40), channel_id=1, source_target_pairs={{0,4},{4,0},{1,5},{5,1},{2,6},{6,2},{3,7},{7,3}} | collective-permute-start | bytes 1572872 | tf_op jit(solution)/shard_map/ppermute | solution.py:175
  24.9 35.4 %copy-start.12 = (bf16[128,16,128]{2,1,0:T(8,128)(2,1)}, bf16[128,16,128]{2,1,0:T(8,128)(2,1)S(1)}, u32[]{:S(2)}) copy-start(bf16[128,16,128]{2,1,0:T(8,128)(2,1)S(1)} %collective-permute-done.4.refs_6_) | copy-start | bytes 1572868
  24.9 15.0 %collective-permute-start.3 = (bf16[128,16,128]{2,1,0:T(8,128)(2,1)S(1)}, bf16[128,16,128]{2,1,0:T(8,128)(2,1)}, u32[]{:S(2)}, u32[]{:S(2)}) collective-permute-start(bf16[128,16,128]{2,1,0:T(8,128)(2,1)S(1)} %bitcast.41), channel_id=1, source_target_pairs={{0,1},{1,0},{2,3},{3,2},{4,5},{5,4},{6,7},{7,6}} | collective-permute-start | bytes 1572872 | tf_op jit(solution)/shard_map/ppermute | solution.py:172
  25.0 35.4 %copy-start.13 = (bf16[128,16,128]{2,1,0:T(8,128)(2,1)}, bf16[128,16,128]{2,1,0:T(8,128)(2,1)S(1)}, u32[]{:S(2)}) copy-start(bf16[128,16,128]{2,1,0:T(8,128)(2,1)S(1)} %collective-permute-done.2.refs_4_) | copy-start | bytes 1572868
  25.0 34.8 %collective-permute-start.11 = (bf16[128,16,128]{2,1,0:T(8,128)(2,1)S(1)}, bf16[128,16,128]{2,1,0:T(8,128)(2,1)}, u32[]{:S(2)}, u32[]{:S(2)}) collective-permute-start(bf16[128,16,128]{2,1,0:T(8,128)(2,1)S(1)} %collective-permute-done.4.refs_6_), channel_id=1, source_target_pairs={{0,4},{4,0},{1,5},{5,1},{2,6},{6,2},{3,7},{7,3}} | collective-permute-start | bytes 1572872 | tf_op jit(solution)/shard_map/ppermute | solution.py:175
  26.5 33.3 %collective-permute-start.5 = (bf16[128,16,128]{2,1,0:T(8,128)(2,1)S(1)}, bf16[128,16,128]{2,1,0:T(8,128)(2,1)}, u32[]{:S(2)}, u32[]{:S(2)}) collective-permute-start(bf16[128,16,128]{2,1,0:T(8,128)(2,1)S(1)} %collective-permute-done.4.refs_6_), channel_id=1, source_target_pairs={{0,1},{1,0},{2,3},{3,2},{4,5},{5,4},{6,7},{7,6}} | collective-permute-start | bytes 1572872 | tf_op jit(solution)/shard_map/ppermute | solution.py:172
  35.3 65.1 %copy-start.10 = (bf16[128,16,128]{2,1,0:T(8,128)(2,1)}, bf16[128,16,128]{2,1,0:T(8,128)(2,1)S(1)}, u32[]{:S(2)}) copy-start(bf16[128,16,128]{2,1,0:T(8,128)(2,1)S(1)} %collective-permute-done.15.refs_6_) | copy-start | bytes 1572868
  35.3 14.2 %collective-permute-start.12 = (bf16[128,16,128]{2,1,0:T(8,128)(2,1)S(1)}, bf16[128,16,128]{2,1,0:T(8,128)(2,1)}, u32[]{:S(2)}, u32[]{:S(2)}) collective-permute-start(bf16[128,16,128]{2,1,0:T(8,128)(2,1)S(1)} %bitcast.42), channel_id=1, source_target_pairs={{0,6},{1,7},{2,4},{3,5},{4,2},{5,3},{6,0},{7,1}} | collective-permute-start | bytes 1572872 | tf_op jit(solution)/shard_map/ppermute | solution.py:179
  37.7 62.7 %copy-start.11 = (bf16[128,16,128]{2,1,0:T(8,128)(2,1)}, bf16[128,16,128]{2,1,0:T(8,128)(2,1)S(1)}, u32[]{:S(2)}) copy-start(bf16[128,16,128]{2,1,0:T(8,128)(2,1)S(1)} %collective-permute-done.9.refs_0_) | copy-start | bytes 1572868
  37.7 22.6 %collective-permute-start.1 = (bf16[128,16,128]{2,1,0:T(8,128)(2,1)}, bf16[128,16,128]{2,1,0:T(8,128)(2,1)}, u32[]{:S(2)}, u32[]{:S(2)}) collective-permute-start(bf16[128,16,128]{2,1,0:T(8,128)(2,1)} %collective-permute-done.refs_0_), channel_id=1, source_target_pairs={{0,1},{1,0},{2,3},{3,2},{4,5},{5,4},{6,7},{7,6}} | collective-permute-start | bytes 1572872 | tf_op jit(solution)/shard_map/ppermute | solution.py:172
  40.0 62.1 %collective-permute-start.16 = (bf16[128,16,128]{2,1,0:T(8,128)(2,1)S(1)}, bf16[128,16,128]{2,1,0:T(8,128)(2,1)}, u32[]{:S(2)}, u32[]{:S(2)}) collective-permute-start(bf16[128,16,128]{2,1,0:T(8,128)(2,1)S(1)} %collective-permute-done.15.refs_6_), channel_id=1, source_target_pairs={{0,1},{1,0},{2,3},{3,2},{4,5},{5,4},{6,7},{7,6}} | collective-permute-start | bytes 1572872 | tf_op jit(solution)/shard_map/ppermute | solution.py:172
  49.5 52.5 %collective-permute-start.10 = (bf16[128,16,128]{2,1,0:T(8,128)(2,1)S(1)}, bf16[128,16,128]{2,1,0:T(8,128)(2,1)}, u32[]{:S(2)}, u32[]{:S(2)}) collective-permute-start(bf16[128,16,128]{2,1,0:T(8,128)(2,1)S(1)} %collective-permute-done.9.refs_0_), channel_id=1, source_target_pairs={{0,1},{1,0},{2,3},{3,2},{4,5},{5,4},{6,7},{7,6}} | collective-permute-start | bytes 1572872 | tf_op jit(solution)/shard_map/ppermute | solution.py:172
  59.8 42.3 %collective-permute-start.14 = (bf16[128,16,128]{2,1,0:T(8,128)(2,1)}, bf16[128,16,128]{2,1,0:T(8,128)(2,1)}, u32[]{:S(2)}, u32[]{:S(2)}) collective-permute-start(bf16[128,16,128]{2,1,0:T(8,128)(2,1)} %collective-permute-done.12.refs_3_), channel_id=1, source_target_pairs={{0,1},{1,0},{2,3},{3,2},{4,5},{5,4},{6,7},{7,6}} | collective-permute-start | bytes 1572872 | tf_op jit(solution)/shard_map/ppermute | solution.py:172
  59.8 42.3 %collective-permute-start.13 = (bf16[128,16,128]{2,1,0:T(8,128)(2,1)}, bf16[128,16,128]{2,1,0:T(8,128)(2,1)}, u32[]{:S(2)}, u32[]{:S(2)}) collective-permute-start(bf16[128,16,128]{2,1,0:T(8,128)(2,1)} %collective-permute-done.11.refs_2_), channel_id=1, source_target_pairs={{0,1},{1,0},{2,3},{3,2},{4,5},{5,4},{6,7},{7,6}} | collective-permute-start | bytes 1572872 | tf_op jit(solution)/shard_map/ppermute | solution.py:172
  100.4 46.4 %copy-start.6 = (f32[128,16,128]{2,1,0:T(8,128)S(1)}, f32[128,16,128]{2,1,0:T(8,128)}, u32[]{:S(2)}) copy-start(f32[128,16,128]{2,1,0:T(8,128)} %get-tuple-element.49) | copy-start | bytes 3145732
  100.5 65.5 %copy-start.4 = (f32[128,16,128]{2,1,0:T(8,128)S(1)}, f32[128,16,128]{2,1,0:T(8,128)}, u32[]{:S(2)}) copy-start(f32[128,16,128]{2,1,0:T(8,128)} %get-tuple-element.51) | copy-start | bytes 3145732
  100.5 45.9 %collective-permute-start.7 = (f32[128,16,128]{2,1,0:T(8,128)}, f32[128,16,128]{2,1,0:T(8,128)S(1)}, u32[]{:S(2)}, u32[]{:S(2)}) collective-permute-start(f32[128,16,128]{2,1,0:T(8,128)} %get-tuple-element.50), channel_id=1, source_target_pairs={{0,4},{4,0},{1,5},{5,1},{2,6},{6,2},{3,7},{7,3}} | collective-permute-start | bytes 3145736 | tf_op jit(solution)/shard_map/ppermute | solution.py:175
  142.3 46.1 %copy-start.14 = (f32[128,16,128]{2,1,0:T(8,128)S(1)}, f32[128,16,128]{2,1,0:T(8,128)}, u32[]{:S(2)}) copy-start(f32[128,16,128]{2,1,0:T(8,128)} %get-tuple-element.64) | copy-start | bytes 3145732
  142.3 46.1 %copy-start.3 = (f32[128,16,128]{2,1,0:T(8,128)S(1)}, f32[128,16,128]{2,1,0:T(8,128)}, u32[]{:S(2)}) copy-start(f32[128,16,128]{2,1,0:T(8,128)} %get-tuple-element.55) | copy-start | bytes 3145732
  142.3 74.0 %copy-start.7 = (f32[128,16,128]{2,1,0:T(8,128)S(1)}, f32[128,16,128]{2,1,0:T(8,128)}, u32[]{:S(2)}) copy-start(f32[128,16,128]{2,1,0:T(8,128)} %get-tuple-element.57) | copy-start | bytes 3145732
  142.3 23.6 %collective-permute-start.17 = (f32[128,16,128]{2,1,0:T(8,128)}, f32[128,16,128]{2,1,0:T(8,128)S(1)}, u32[]{:S(2)}, u32[]{:S(2)}) collective-permute-start(f32[128,16,128]{2,1,0:T(8,128)} %get-tuple-element.54), channel_id=1, source_target_pairs={{0,4},{4,0},{1,5},{5,1},{2,6},{6,2},{3,7},{7,3}} | collective-permute-start | bytes 3145736 | tf_op jit(solution)/shard_map/ppermute | solution.py:175
  142.8 45.6 %collective-permute-start.19 = (f32[128,16,128]{2,1,0:T(8,128)}, f32[128,16,128]{2,1,0:T(8,128)S(1)}, u32[]{:S(2)}, u32[]{:S(2)}) collective-permute-start(f32[128,16,128]{2,1,0:T(8,128)} %get-tuple-element.56), channel_id=1, source_target_pairs={{0,4},{4,0},{1,5},{5,1},{2,6},{6,2},{3,7},{7,3}} | collective-permute-start | bytes 3145736 | tf_op jit(solution)/shard_map/ppermute | solution.py:175
  144.4 66.5 %collective-permute-start.21 = (f32[128,16,128]{2,1,0:T(8,128)}, f32[128,16,128]{2,1,0:T(8,128)S(1)}, u32[]{:S(2)}, u32[]{:S(2)}) collective-permute-start(f32[128,16,128]{2,1,0:T(8,128)} %get-tuple-element.58), channel_id=1, source_target_pairs={{0,4},{4,0},{1,5},{5,1},{2,6},{6,2},{3,7},{7,3}} | collective-permute-start | bytes 3145736 | tf_op jit(solution)/shard_map/ppermute | solution.py:175
  144.8 88.5 %collective-permute-start.23 = (f32[128,16,128]{2,1,0:T(8,128)}, f32[128,16,128]{2,1,0:T(8,128)S(1)}, u32[]{:S(2)}, u32[]{:S(2)}) collective-permute-start(f32[128,16,128]{2,1,0:T(8,128)} %get-tuple-element.60), channel_id=1, source_target_pairs={{0,4},{4,0},{1,5},{5,1},{2,6},{6,2},{3,7},{7,3}} | collective-permute-start | bytes 3145736 | tf_op jit(solution)/shard_map/ppermute | solution.py:175
  146.4 113.2 %copy-start.5 = (f32[128,16,128]{2,1,0:T(8,128)S(1)}, f32[128,16,128]{2,1,0:T(8,128)}, u32[]{:S(2)}) copy-start(f32[128,16,128]{2,1,0:T(8,128)} %get-tuple-element.59) | copy-start | bytes 3145732
  146.4 109.4 %collective-permute-start.25 = (f32[128,16,128]{2,1,0:T(8,128)}, f32[128,16,128]{2,1,0:T(8,128)S(1)}, u32[]{:S(2)}, u32[]{:S(2)}) collective-permute-start(f32[128,16,128]{2,1,0:T(8,128)} %get-tuple-element.62), channel_id=1, source_target_pairs={{0,4},{4,0},{1,5},{5,1},{2,6},{6,2},{3,7},{7,3}} | collective-permute-start | bytes 3145736 | tf_op jit(solution)/shard_map/ppermute | solution.py:175
  147.0 112.7 %copy-start.2 = (f32[128,16,128]{2,1,0:T(8,128)S(1)}, f32[128,16,128]{2,1,0:T(8,128)}, u32[]{:S(2)}) copy-start(f32[128,16,128]{2,1,0:T(8,128)} %get-tuple-element.61) | copy-start | bytes 3145732
  166.0 112.4 %collective-permute-start.6 = (f32[128,16,128]{2,1,0:T(8,128)}, f32[128,16,128]{2,1,0:T(8,128)S(1)}, u32[]{:S(2)}, u32[]{:S(2)}) collective-permute-start(f32[128,16,128]{2,1,0:T(8,128)} %get-tuple-element.48), channel_id=1, source_target_pairs={{0,4},{4,0},{1,5},{5,1},{2,6},{6,2},{3,7},{7,3}} | collective-permute-start | bytes 3145736 | tf_op jit(solution)/shard_map/ppermute | solution.py:175
  188.4 96.6 %copy-start.9 = (f32[128,16,128]{2,1,0:T(8,128)S(1)}, f32[128,16,128]{2,1,0:T(8,128)}, u32[]{:S(2)}) copy-start(f32[128,16,128]{2,1,0:T(8,128)} %get-tuple-element.47) | copy-start | bytes 3145732
  188.4 112.3 %collective-permute-start.27 = (f32[128,16,128]{2,1,0:T(8,128)S(1)}, f32[128,16,128]{2,1,0:T(8,128)S(1)}, u32[]{:S(2)}, u32[]{:S(2)}) collective-permute-start(f32[128,16,128]{2,1,0:T(8,128)S(1)} %copy-done.14), channel_id=1, source_target_pairs={{0,4},{4,0},{1,5},{5,1},{2,6},{6,2},{3,7},{7,3}} | collective-permute-start | bytes 3145736 | tf_op jit(solution)/shard_map/ppermute | solution.py:175
  210.9 71.7 %collective-permute-start.8 = (bf16[128,16,128]{2,1,0:T(8,128)(2,1)S(1)}, bf16[128,16,128]{2,1,0:T(8,128)(2,1)S(1)}, u32[]{:S(2)}, u32[]{:S(2)}) collective-permute-start(bf16[128,16,128]{2,1,0:T(8,128)(2,1)S(1)} %add_convert_fusion.8), channel_id=1, source_target_pairs={{0,1},{1,0},{2,3},{3,2},{4,5},{5,4},{6,7},{7,6}} | collective-permute-start | bytes 1572872 | tf_op jit(solution)/shard_map/ppermute | solution.py:172
  233.4 51.7 %collective-permute-start.18 = (bf16[128,16,128]{2,1,0:T(8,128)(2,1)S(1)}, bf16[128,16,128]{2,1,0:T(8,128)(2,1)S(1)}, u32[]{:S(2)}, u32[]{:S(2)}) collective-permute-start(bf16[128,16,128]{2,1,0:T(8,128)(2,1)S(1)} %add_convert_fusion.7), channel_id=1, source_target_pairs={{0,2},{1,3},{2,0},{3,1},{4,6},{5,7},{6,4},{7,5}} | collective-permute-start | bytes 1572872 | tf_op jit(solution)/shard_map/ppermute | solution.py:172
  255.8 29.2 %collective-permute-start.20 = (bf16[128,16,128]{2,1,0:T(8,128)(2,1)S(1)}, bf16[128,16,128]{2,1,0:T(8,128)(2,1)S(1)}, u32[]{:S(2)}, u32[]{:S(2)}) collective-permute-start(bf16[128,16,128]{2,1,0:T(8,128)(2,1)S(1)} %add_convert_fusion.6), channel_id=1, source_target_pairs={{0,3},{1,2},{2,1},{3,0},{4,7},{5,6},{6,5},{7,4}} | collective-permute-start | bytes 1572872 | tf_op jit(solution)/shard_map/ppermute | solution.py:172
  259.5 47.0 %copy-start.8 = (f32[128,16,128]{2,1,0:T(8,128)S(1)}, f32[128,16,128]{2,1,0:T(8,128)}, u32[]{:S(2)}) copy-start(f32[128,16,128]{2,1,0:T(8,128)} %get-tuple-element.63) | copy-start | bytes 3145732
  278.3 22.5 %collective-permute-start.22 = (bf16[128,16,128]{2,1,0:T(8,128)(2,1)S(1)}, bf16[128,16,128]{2,1,0:T(8,128)(2,1)S(1)}, u32[]{:S(2)}, u32[]{:S(2)}) collective-permute-start(bf16[128,16,128]{2,1,0:T(8,128)(2,1)S(1)} %add_convert_fusion.4), channel_id=1, source_target_pairs={{0,2},{1,3},{2,0},{3,1},{4,6},{5,7},{6,4},{7,5}} | collective-permute-start | bytes 1572872 | tf_op jit(solution)/shard_map/ppermute | solution.py:172
  282.6 24.0 %collective-permute-start.24 = (bf16[128,16,128]{2,1,0:T(8,128)(2,1)S(1)}, bf16[128,16,128]{2,1,0:T(8,128)(2,1)S(1)}, u32[]{:S(2)}, u32[]{:S(2)}) collective-permute-start(bf16[128,16,128]{2,1,0:T(8,128)(2,1)S(1)} %add_convert_fusion.3), channel_id=1, source_target_pairs={{0,3},{1,2},{2,1},{3,0},{4,7},{5,6},{6,5},{7,4}} | collective-permute-start | bytes 1572872 | tf_op jit(solution)/shard_map/ppermute | solution.py:172
  285.0 21.6 %collective-permute-start.26 = (bf16[128,16,128]{2,1,0:T(8,128)(2,1)S(1)}, bf16[128,16,128]{2,1,0:T(8,128)(2,1)S(1)}, u32[]{:S(2)}, u32[]{:S(2)}) collective-permute-start(bf16[128,16,128]{2,1,0:T(8,128)(2,1)S(1)} %add_convert_fusion.2), channel_id=1, source_target_pairs={{0,1},{1,0},{2,3},{3,2},{4,5},{5,4},{6,7},{7,6}} | collective-permute-start | bytes 1572872 | tf_op jit(solution)/shard_map/ppermute | solution.py:172
